TPU v7x, 8 devices: a whole 2x2x1 slice. The times are simulated.
8 devices in a mesh: dp: 2 (over z, y), cp: 4 (over x, core).
Axes of the slice: x: 2, y: 2, z: 1, core: 2. Of those that a mesh axis runs over, the one named last changes fastest.
Arguments:
- vis_feat: bfloat16 [16, 4096, 1152], P(('dp', 'cp')), parts along dimension 0
- text_emb: bfloat16 [8192, 2560], P(('dp', 'cp')), parts along dimension 0
- img_pos: int32 [16], P('dp'), parts along dimension 0
- grad_y: bfloat16 [8192, 2560], P(('dp', 'cp')), parts along dimension 0
- pn_gain: bfloat16 [1152], replicated
- w_proj: bfloat16 [1152, 2560], replicated
- pre_gain: bfloat16 [2560], replicated
- w_query: bfloat16 [2560, 2048], replicated
- w_key: bfloat16 [2560, 1024], replicated
- w_value: bfloat16 [2560, 1024], replicated
- q_gain: bfloat16 [256], replicated
- k_gain: bfloat16 [256], replicated
- w_out: bfloat16 [2048, 2560], replicated
- post_gain: bfloat16 [2560], replicated
Outputs:
- output 1: bfloat16 [8192, 2560], P(('dp', 'cp')), parts along dimension 0
- output 2: bfloat16 [8192, 2560], P(('dp', 'cp')), parts along dimension 0
- output 3: bfloat16 [16, 4096, 1152], P(('dp', 'cp')), parts along dimension 0
- output 4: bfloat16 [2304], P('dp'), parts along dimension 0
- output 5: bfloat16 [2304, 2560], P('dp'), parts along dimension 0
- output 6: bfloat16 [5120], P('dp'), parts along dimension 0
- output 7: bfloat16 [5120, 2048], P('dp'), parts along dimension 0
- output 8: bfloat16 [5120, 1024], P('dp'), parts along dimension 0
- output 9: bfloat16 [5120, 1024], P('dp'), parts along dimension 0
- output 10: bfloat16 [512], P('dp'), parts along dimension 0
- output 11: bfloat16 [512], P('dp'), parts along dimension 0
- output 12: bfloat16 [4096, 2560], P('dp'), parts along dimension 0
- output 13: bfloat16 [5120], P('dp'), parts along dimension 0
There are 2 independent parts. A program takes and returns all parts, laid end to end along the dimension named above; an argument that names none is the same for every part.
All inputs are finite; a program needn't handle non-finite values.
Results may differ from a plain program's by a relative error of at most 0.02.
Values are sent between devices in bfloat16 or wider.
A program may use at most 1 GiB of HBM per device.

v0:
```python
import functools
import jax
import jax.numpy as jnp
from jax import lax
from jax.experimental import pallas as pl
from jax.experimental.pallas import tpu as pltpu
from jax.sharding import PartitionSpec as P


GRID = 64
POOL = 4
SIDE = GRID // POOL
BLK = SIDE * SIDE
HD = 256
HD2 = 2 * HD
HD3 = 3 * HD
NBUF = 10
ROWS = 1024
CHIP = 2 * ROWS
SEQ = 2 * CHIP
LANES = 128
YES = True
ALL = ...
ONE = 1.0
EPS = 1e-6
ROPE_BASE = 1000000.0
ROPE_SCALE = 8.0
NEG_BIG = -1e30
LOG2E = 1.4426950408889634
BF = jnp.bfloat16
F32 = jnp.float32
FAR = 1 << 20
SLOT = (0, 2, 1, 3)
VMEM_MAX = 67043328

XPERM = [(0, 2), (2, 0), (1, 3), (3, 1)]
SPERM = [(0, 1), (1, 0), (2, 3), (3, 2)]


def dot(a, b):
    return lax.dot_general(a, b, (((1,), (0,)), ((), ())), preferred_element_type=F32)


def dot_nt(a, b):
    return lax.dot_general(a, b, (((1,), (1,)), ((), ())), preferred_element_type=F32)


def dot_tn(a, b):
    return lax.dot_general(a, b, (((0,), (0,)), ((), ())), preferred_element_type=F32)


def params(n_grid, **kw):
    return pltpu.CompilerParams(dimension_semantics=("arbitrary",) * n_grid, vmem_limit_bytes=kw.pop("vmem", VMEM_MAX - (1 << 20)), **kw)


def cost(flops, nbytes):
    return pl.CostEstimate(flops=int(flops), bytes_accessed=int(nbytes), transcendentals=0)


def const_spec(shape):
    return pl.BlockSpec(shape, lambda *a: (0,) * len(shape), pipeline_mode=pl.Buffered(1))


ANY = pl.BlockSpec(memory_space=pl.ANY)


def const_out(shape):
    return pl.BlockSpec(shape, lambda *a: (0,) * len(shape))


def pool_kernel(vis_ref, gain_ref, pooled_ref, normed_ref):
    row = lax.broadcasted_iota(jnp.int32, (GRID, ROWS), 0)
    src = lax.broadcasted_iota(jnp.int32, (GRID, ROWS), 1)
    hit = (row // SIDE == src // HD) & (row % SIDE == (src % GRID) // POOL)
    mask = jnp.where(hit, ONE, 0.0).astype(BF)
    pooled = (dot(mask, vis_ref[0]) * (ONE / 16.0)).astype(BF)
    pooled_ref[ALL] = pooled
    wide = pooled.astype(F32)
    rs = lax.rsqrt(jnp.mean(wide * wide, axis=1, keepdims=YES) + EPS)
    normed_ref[ALL] = (wide * rs * (ONE + gain_ref[ALL])).astype(BF)


def pool_call(vis, gain):
    n, _, dv = vis.shape
    return pl.pallas_call(
        pool_kernel,
        grid=(n * POOL,),
        in_specs=[pl.BlockSpec((1, ROWS, dv), lambda i: (i // POOL, i % POOL, 0)), const_spec((1, dv))],
        out_specs=[pl.BlockSpec((GRID, dv), lambda i: (i, 0))] * 2,
        out_shape=[jax.ShapeDtypeStruct((n * BLK, dv), BF)] * 2,
        compiler_params=params(1),
        cost_estimate=cost(2 * HD2 * ROWS * dv, vis.size * 2),
        name="pool",
    )(vis, gain)


def merge_kernel(tab, sc, soft, text, gain, x_ref, h_ref):
    b = sc[0] * POOL + pl.program_id(0)
    ia, da, ib, db = tab[POOL * b], tab[POOL * b + 1], tab[POOL * b + 2], tab[POOL * b + 3]
    some = (da < FAR) | (db < FAR)

    @pl.when(some)
    def _():
        row = lax.broadcasted_iota(jnp.int32, (HD, HD), 0)
        col = lax.broadcasted_iota(jnp.int32, (HD, HD), 1)
        pa = jnp.where(col == row + da, ONE, 0.0).astype(BF)
        pb = jnp.where(col == row + db, ONE, 0.0).astype(BF)
        sa = soft[pl.ds(pl.multiple_of(ia * HD, HD), HD), :]
        sb = soft[pl.ds(pl.multiple_of(ib * HD, HD), HD), :]
        val = (dot(pa, sa) + dot(pb, sb)).astype(BF)
        r1 = lax.broadcasted_iota(jnp.int32, (HD, 1), 0)
        ina = (r1 + da >= 0) & (r1 + da < HD)
        inb = (r1 + db >= 0) & (r1 + db < HD)
        x_ref[ALL] = jnp.where(ina | inb, val, text[ALL])

    @pl.when(jnp.logical_not(some))
    def _():
        x_ref[ALL] = text[ALL]

    xv = x_ref[ALL].astype(F32)
    rs = lax.rsqrt(jnp.mean(xv * xv, axis=1, keepdims=YES) + EPS)
    h_ref[ALL] = (xv * rs * (ONE + gain[ALL])).astype(BF)


def merge_call(tab, rr, soft, text, gain):
    rows, d = text.shape
    spec = pl.BlockSpec((HD, d), lambda i, *_: (i, 0))
    return pl.pallas_call(
        merge_kernel,
        grid_spec=pltpu.PrefetchScalarGridSpec(
            num_scalar_prefetch=2,
            grid=(rows // HD,),
            in_specs=[const_spec(soft.shape), spec, const_spec((1, d))],
            out_specs=[spec, spec],
        ),
        out_shape=[jax.ShapeDtypeStruct((rows, d), BF)] * 2,
        compiler_params=params(1),
        cost_estimate=cost(2 * rows * HD2 * d, (rows * 3 + soft.shape[0]) * d * 2),
        name="merge",
    )(tab, rr, soft, text, gain)


def rope_fwd(raw, gain, cos, sin):
    rs = lax.rsqrt(jnp.mean(raw * raw, axis=1, keepdims=YES) + EPS)
    n = raw * rs * (ONE + gain)
    a, b = n[:, :LANES], n[:, LANES:]
    return jnp.concatenate([a * cos - b * sin, b * cos + a * sin], axis=1)


def qkv_kernel(sc, ha, hb, wq, wk, wv, qg, kg, cos_ref, sin_ref, *rest):
    outs = rest[-NBUF:]
    q_o, qr_o, k_o, kr_o, v_o = outs[0:2], outs[2:POOL], outs[POOL:6], outs[6:8], outs[8:NBUF]
    hid = jnp.where(pl.program_id(0) < 2, ha[ALL], hb[ALL])
    cos, sin = cos_ref[ALL], sin_ref[ALL]
    for g in range(2):
        aq = dot(hid, wq[:, HD2 * g : HD2 * g + HD2]).astype(BF)
        qr_o[g][ALL] = aq
        for h in range(2):
            raw = aq[:, HD * h : HD * h + HD].astype(F32)
            q_o[g][:, HD * h : HD * h + HD] = (rope_fwd(raw, qg[ALL], cos, sin) * 0.0625).astype(BF)
        ak = dot(hid, wk[:, HD * g : HD * g + HD]).astype(BF)
        kr_o[g][ALL] = ak
        k_o[g][ALL] = rope_fwd(ak.astype(F32), kg[ALL], cos, sin).astype(BF)
        v_o[g][ALL] = dot(hid, wv[:, HD * g : HD * g + HD]).astype(BF)


def qkv_call(sc, ha, hb, wq, wk, wv, qg, kg, cos, sin, bufs):
    d = ha.shape[1]
    rows = HD2

    def outrow(i, s):
        return s[0] * POOL + jnp.where(i < 2, s[1] * 2 + i, (1 - s[1]) * 2 + i - 2)

    def ospec(w):
        return pl.BlockSpec((rows, w), lambda i, s: (outrow(i, s), 0))

    one = dict(pipeline_mode=pl.Buffered(1))
    widths = [HD2, HD2, HD2, HD2, HD, HD, HD, HD, HD, HD]
    in_specs = [
        pl.BlockSpec((rows, d), lambda i, s: (jnp.minimum(i, 1), 0)),
        pl.BlockSpec((rows, d), lambda i, s: (jnp.maximum(i - 2, 0), 0)),
        pl.BlockSpec((d, ROWS), lambda i, s: (0, s[1]), **one),
        pl.BlockSpec((d, HD2), lambda i, s: (0, s[1]), **one),
        pl.BlockSpec((d, HD2), lambda i, s: (0, s[1]), **one),
        const_spec((1, HD)),
        const_spec((1, HD)),
        ospec(LANES),
        ospec(LANES),
    ]
    args = [sc, ha, hb, wq, wk, wv, qg, kg, cos, sin]
    alias = {}
    if bufs:
        alias = {len(args) + n: n for n in range(NBUF)}
        in_specs += [ANY] * NBUF
        args += list(bufs)
    seq = POOL * ha.shape[0]
    return pl.pallas_call(
        qkv_kernel,
        grid_spec=pltpu.PrefetchScalarGridSpec(
            num_scalar_prefetch=1, grid=(POOL,), in_specs=in_specs, out_specs=[ospec(w) for w in widths]
        ),
        out_shape=[jax.ShapeDtypeStruct((seq, w), BF) for w in widths],
        input_output_aliases=alias,
        compiler_params=params(1),
        cost_estimate=cost(2 * CHIP * d * CHIP, CHIP * (d + 3584) * 2 + d * CHIP * 2),
        name="qkv",
    )(*args)


QB = 512
KB = 512


def fwd_kernel(nkv, q_ref, k_ref, v_ref, bs_ref, o_ref, lse_ref, m_s, l_s, acc_s):
    i = pl.program_id(0)
    m_s[ALL] = jnp.full(m_s.shape, NEG_BIG, F32)
    l_s[ALL] = jnp.zeros(l_s.shape, F32)
    acc_s[ALL] = jnp.zeros(acc_s.shape, F32)

    def step(j, masked):
        off = pl.multiple_of(j * KB, KB)
        kb = k_ref[pl.ds(off, KB), :]
        vb = v_ref[pl.ds(off, KB), :]
        if masked:
            qpos = i * QB + lax.broadcasted_iota(jnp.int32, (QB, KB), 0)
            kpos = j * KB + lax.broadcasted_iota(jnp.int32, (QB, KB), 1)
            rel = kpos - bs_ref[ALL]
            vis = (kpos <= qpos) | ((rel >= 0) & (rel < BLK))
        ss = [dot_nt(q_ref[:, HD * h : HD * h + HD], kb) for h in range(2)]
        for h in range(2):
            s = ss[h]
            if masked:
                s = jnp.where(vis, s, NEG_BIG)
            parts = [s[:, LANES * t : LANES * t + LANES] for t in range(KB // LANES)]
            mx = functools.reduce(jnp.maximum, parts)
            mx = jnp.broadcast_to(jnp.max(mx, axis=1, keepdims=YES), (QB, LANES))
            m_old = m_s[h]
            m_new = jnp.maximum(m_old, mx)
            alpha = jnp.exp2((m_old - m_new) * LOG2E)
            ps = [jnp.exp2((t - m_new) * LOG2E) for t in parts]
            l_s[h] = l_s[h] * alpha + functools.reduce(jnp.add, ps)
            m_s[h] = m_new
            p = jnp.concatenate([t.astype(BF) for t in ps], axis=1)
            acc_s[h] = acc_s[h] * jnp.concatenate([alpha, alpha], axis=1) + dot(p, vb)

    lax.fori_loop(0, i, lambda j, c: (step(j, False), c)[1], 0)
    step(i, YES)

    @pl.when(nkv[i] > i + 1)
    def _():
        step(i + 1, YES)

    for h in range(2):
        l = jnp.broadcast_to(jnp.sum(l_s[h], axis=1, keepdims=YES), (QB, LANES))
        inv = ONE / l
        o_ref[:, HD * h : HD * h + HD] = (acc_s[h] * jnp.concatenate([inv, inv], axis=1)).astype(BF)
        lse = m_s[h] * LOG2E + jnp.log2(l)
        lse_ref[0, h : h + 1, :] = jnp.transpose(lse)[0:1, :]


def fwd_call(nkv, q, k, v, bs_col):
    seq = q.shape[0]
    n = seq // QB
    return pl.pallas_call(
        fwd_kernel,
        grid_spec=pltpu.PrefetchScalarGridSpec(
            num_scalar_prefetch=1,
            grid=(n,),
            in_specs=[
                pl.BlockSpec((QB, HD2), lambda i, *_: (i, 0)),
                const_spec((seq, HD)),
                const_spec((seq, HD)),
                pl.BlockSpec((QB, 1), lambda i, *_: (i, 0)),
            ],
            out_specs=[pl.BlockSpec((QB, HD2), lambda i, *_: (i, 0)), pl.BlockSpec((1, 2, QB), lambda i, *_: (i, 0, 0))],
            scratch_shapes=[pltpu.VMEM((2, QB, LANES), F32), pltpu.VMEM((2, QB, LANES), F32), pltpu.VMEM((2, QB, HD), F32)],
        ),
        out_shape=[jax.ShapeDtypeStruct((seq, HD2), BF), jax.ShapeDtypeStruct((n, 2, QB), F32)],
        compiler_params=params(1),
        cost_estimate=cost(2 * 2 * 2 * seq * seq * HD * 0.7, seq * 1536 * 2),
        name="attn_fwd",
    )(nkv, q, k, v, bs_col)


def out_kernel(sc, oo0, oo1, os0, os1, wo, dy_ref, gain, *rest):
    x_ref, y_ref = rest[:2] if len(rest) == 8 else (None, None)
    dp_ref, da_o0, da_o1, da_s0, da_s1, gp_ref = rest[-6:]
    c = sc[1]
    own = pl.multiple_of(c * ROWS, ROWS)
    sib = pl.multiple_of((1 - c) * ROWS, ROWS)
    a = dot(oo0[ALL], wo[pl.ds(own, HD2), :])
    a = a + dot(oo1[ALL], wo[pl.ds(own + HD2, HD2), :])
    a = a + dot(os0[ALL], wo[pl.ds(sib, HD2), :])
    a = a + dot(os1[ALL], wo[pl.ds(sib + HD2, HD2), :])
    a = a.astype(BF).astype(F32)
    rs = lax.rsqrt(jnp.mean(a * a, axis=1, keepdims=YES) + EPS)
    g1 = ONE + gain[ALL]
    n = a * rs
    if y_ref is not None:
        y_ref[ALL] = (x_ref[ALL].astype(F32) + n * g1).astype(BF)
    dy = dy_ref[ALL].astype(F32)
    dyn = dy * n

    @pl.when(pl.program_id(0) == 0)
    def _():
        gp_ref[ALL] = jnp.zeros_like(gp_ref)

    gp_ref[ALL] += jnp.sum(dyn, axis=0, keepdims=YES)
    mean = jnp.mean(dyn * g1, axis=1, keepdims=YES)
    dp = ((dy * g1 - n * mean) * rs).astype(BF)
    dp_ref[ALL] = dp
    da_o0[ALL] = dot_nt(dp, wo[pl.ds(own, HD2), :]).astype(BF)
    da_o1[ALL] = dot_nt(dp, wo[pl.ds(own + HD2, HD2), :]).astype(BF)
    da_s0[ALL] = dot_nt(dp, wo[pl.ds(sib, HD2), :]).astype(BF)
    da_s1[ALL] = dot_nt(dp, wo[pl.ds(sib + HD2, HD2), :]).astype(BF)


def out_call(sc, oo, osib, wo, dy, gain, x=()):
    rows, d = dy.shape
    rb = HD
    nb = rows // rb

    def orow(i, s):
        return (s[0] * 2 + s[1]) * nb + i

    ospec = pl.BlockSpec((rb, HD2), lambda i, s: (orow(i, s), 0))
    rspec = pl.BlockSpec((rb, d), lambda i, s: (i, 0))
    pspec = pl.BlockSpec((rb, HD2), lambda i, s: (i, 0))
    extra = len(x)
    return pl.pallas_call(
        out_kernel,
        grid_spec=pltpu.PrefetchScalarGridSpec(
            num_scalar_prefetch=1,
            grid=(nb,),
            in_specs=[ospec] * POOL + [const_spec(wo.shape), rspec, const_spec((1, d))] + [rspec] * extra,
            out_specs=[rspec] * (1 + extra) + [pspec] * POOL + [const_out((1, d))],
        ),
        out_shape=[jax.ShapeDtypeStruct((rows, d), BF)] * (1 + extra)
        + [jax.ShapeDtypeStruct((rows, HD2), BF)] * POOL
        + [jax.ShapeDtypeStruct((1, d), F32)],
        compiler_params=params(1),
        cost_estimate=cost(POOL * rows * d * CHIP, rows * d * 2 * 5 + wo.size * 2),
        name="out_proj",
    )(sc, oo[0], oo[1], osib[0], osib[1], wo, dy, gain, *x)


def rope_norm_bwd(dy, raw, gain, cos, sin):
    d1, d2 = dy[:, :LANES], dy[:, LANES:]
    dn = jnp.concatenate([d1 * cos + d2 * sin, d2 * cos - d1 * sin], axis=1)
    rs = lax.rsqrt(jnp.mean(raw * raw, axis=1, keepdims=YES) + EPS)
    n = raw * rs
    dnn = dn * n
    gg = jnp.sum(dnn, axis=0, keepdims=YES)
    mean = jnp.mean(dnn * (ONE + gain), axis=1, keepdims=YES)
    return ((dn * (ONE + gain) - n * mean) * rs).astype(BF), gg


def bwd_kernel(
    sc, q_ref, do_a, do_b, do_c, do_d, o_ref, k_ref, v_ref, lse_ref, bs_ref, qr_ref, kr_ref, cos_ref, sin_ref, qg, kg,
    out_ref, gq_ref, gk_ref, do_s, dl_s, dq_s, dk_s, dv_s, sem,
):
    j = pl.program_id(0)
    nj = pl.num_programs(0)

    @pl.when(j == 0)
    def _():
        cps = []
        for n, src in enumerate((do_a, do_b, do_c, do_d)):
            row = pl.multiple_of((sc[0] ^ SLOT[n]) * ROWS, ROWS)
            cps.append(pltpu.make_async_copy(src, do_s.at[pl.ds(row, ROWS), :], sem.at[n]))
        for cp in cps:
            cp.start()
        dq_s[ALL] = jnp.zeros_like(dq_s)
        gq_ref[ALL] = jnp.zeros_like(gq_ref)
        gk_ref[ALL] = jnp.zeros_like(gk_ref)
        for cp in cps:
            cp.wait()

        def delta(i, carry):
            off = pl.multiple_of(i * QB, QB)
            pr = do_s[pl.ds(off, QB), :].astype(F32) * o_ref[pl.ds(off, QB), :].astype(F32)
            for h in range(2):
                col = jnp.sum(pr[:, HD * h : HD * h + HD], axis=1, keepdims=YES)
                dl_s[i, h : h + 1, :] = jnp.transpose(jnp.broadcast_to(col, (QB, LANES)))[0:1, :]
            return carry

        lax.fori_loop(0, SEQ // QB, delta, 0)

    dk_s[ALL] = jnp.zeros_like(dk_s)
    dv_s[ALL] = jnp.zeros_like(dv_s)
    kb = k_ref[ALL]
    vb = v_ref[ALL]

    def step(i, masked):
        off = pl.multiple_of(i * QB, QB)
        if masked:
            kpos = j * KB + lax.broadcasted_iota(jnp.int32, (KB, QB), 0)
            qpos = i * QB + lax.broadcasted_iota(jnp.int32, (KB, QB), 1)
            rel = kpos - bs_ref[i]
            vis = (kpos <= qpos) | ((rel >= 0) & (rel < BLK))
        qs = [q_ref[pl.ds(off, QB), HD * h : HD * h + HD] for h in range(2)]
        dos = [do_s[pl.ds(off, QB), HD * h : HD * h + HD] for h in range(2)]
        st = [dot_nt(kb, qs[h]) for h in range(2)]
        dpt = [dot_nt(vb, dos[h]) for h in range(2)]
        for h in range(2):
            pt = jnp.exp2(st[h] * LOG2E - lse_ref[i, h : h + 1, :])
            if masked:
                pt = jnp.where(vis, pt, 0.0)
            dst = (pt * (dpt[h] - dl_s[i, h : h + 1, :])).astype(BF)
            dv_s[ALL] += dot(pt.astype(BF), dos[h])
            dk_s[ALL] += dot(dst, qs[h])
            dq_s[pl.ds(off, QB), HD * h : HD * h + HD] += dot_tn(dst, kb)

    @pl.when(sc[1 + j] < j)
    def _():
        step(jnp.maximum(j - 1, 0), YES)

    step(j, YES)
    lax.fori_loop(j + 1, nj, lambda i, cr: (step(i, False), cr)[1], 0)

    koff = pl.multiple_of(j * KB, KB)
    dk, gk = rope_norm_bwd(
        dk_s[ALL].astype(BF).astype(F32), kr_ref[ALL].astype(F32), kg[ALL], cos_ref[pl.ds(koff, KB), :], sin_ref[pl.ds(koff, KB), :]
    )
    gk_ref[ALL] += gk
    out_ref[pl.ds(koff, KB), HD2:HD3] = dk
    out_ref[pl.ds(koff, KB), HD3:ROWS] = dv_s[ALL].astype(BF)

    @pl.when(j == nj - 1)
    def _():
        def fin(i, carry):
            off = pl.multiple_of(i * HD, HD)
            cos, sin = cos_ref[pl.ds(off, HD), :], sin_ref[pl.ds(off, HD), :]
            for h in range(2):
                sl = slice(HD * h, HD * h + HD)
                dq = (dq_s[pl.ds(off, HD), sl] * 0.0625).astype(BF).astype(F32)
                dqr, gq = rope_norm_bwd(dq, qr_ref[pl.ds(off, HD), sl].astype(F32), qg[ALL], cos, sin)
                gq_ref[ALL] += gq
                out_ref[pl.ds(off, HD), sl] = dqr
            return carry

        lax.fori_loop(0, SEQ // HD, fin, 0)


def bwd_call(sc, q, dos, o, k, v, lse, bs_row, qr, kr, cos, sin, qg, kg):
    seq = q.shape[0]
    nj = seq // KB
    return pl.pallas_call(
        bwd_kernel,
        grid_spec=pltpu.PrefetchScalarGridSpec(
            num_scalar_prefetch=1,
            grid=(nj,),
            in_specs=[
                const_spec((seq, HD2)),
                ANY,
                ANY,
                ANY,
                ANY,
                const_spec((seq, HD2)),
                pl.BlockSpec((KB, HD), lambda j, *_: (j, 0)),
                pl.BlockSpec((KB, HD), lambda j, *_: (j, 0)),
                const_spec(lse.shape),
                const_spec(bs_row.shape),
                const_spec((seq, HD2)),
                pl.BlockSpec((KB, HD), lambda j, *_: (j, 0)),
                const_spec((seq, LANES)),
                const_spec((seq, LANES)),
                const_spec((1, HD)),
                const_spec((1, HD)),
            ],
            out_specs=[
                pl.BlockSpec((seq, ROWS), lambda j, *_: (0, 0)),
                pl.BlockSpec((1, HD), lambda j, *_: (0, 0)),
                pl.BlockSpec((1, HD), lambda j, *_: (0, 0)),
            ],
            scratch_shapes=[
                pltpu.VMEM((seq, HD2), BF),
                pltpu.VMEM((seq // QB, 2, QB), F32),
                pltpu.VMEM((seq, HD2), F32),
                pltpu.VMEM((KB, HD), F32),
                pltpu.VMEM((KB, HD), F32),
                pltpu.SemaphoreType.DMA((POOL,)),
            ],
        ),
        out_shape=[
            jax.ShapeDtypeStruct((seq, ROWS), BF),
            jax.ShapeDtypeStruct((1, HD), F32),
            jax.ShapeDtypeStruct((1, HD), F32),
        ],
        compiler_params=params(1),
        cost_estimate=cost(5 * 2 * 2 * seq * seq * HD * 0.6, seq * 4000 * 2),
        name="attn_bwd",
    )(sc, q, *dos, o, k, v, lse, bs_row, qr, kr, cos, sin, qg, kg)


def gwo_kernel(sc, o0, o1, dp0, dp1, dp2, dp3, out_ref, full_ref, acc):
    s = pl.program_id(0)
    o = jnp.where(sc[0] == 0, o0[ALL], o1[ALL])

    @pl.when(s == 0)
    def _():
        acc[ALL] = jnp.zeros_like(acc)

    for n, ref in enumerate((dp0, dp1, dp2, dp3)):

        @pl.when(s // 2 == n)
        def _():
            acc[ALL] += dot_tn(o, ref[ALL])

    @pl.when(s == pl.num_programs(0) - 1)
    def _():
        out_ref[ALL] = acc[ALL].astype(BF)
        full_ref[ALL] = acc[ALL].astype(BF)


def gwo_call(sc, o0, o1, dps):
    seq = o0.shape[0]
    d = dps[0].shape[1]
    ospec = pl.BlockSpec((HD2, HD2), lambda s, p: (p[3 + s // 2] * 2 + s % 2, 0))
    dspecs = [pl.BlockSpec((HD2, d), lambda s, p, n=n: (jnp.clip(s - 2 * n, 0, 1), 0)) for n in range(POOL)]
    return pl.pallas_call(
        gwo_kernel,
        grid_spec=pltpu.PrefetchScalarGridSpec(
            num_scalar_prefetch=1,
            grid=(8,),
            in_specs=[ospec, ospec] + dspecs,
            out_specs=[const_out((HD2, d)), pl.BlockSpec((HD2, d), lambda s, p: (2 * p[1] + p[0], 0))],
            scratch_shapes=[pltpu.VMEM((HD2, d), F32)],
        ),
        out_shape=[jax.ShapeDtypeStruct((HD2, d), BF), jax.ShapeDtypeStruct((CHIP, d), BF)],
        compiler_params=params(1),
        cost_estimate=cost(2 * seq * HD2 * d, seq * (d + ROWS) * 2),
        name="grad_wo",
    )(sc, o0, o1, *dps)


def gqkv_kernel(sc, h0, h1, h2, h3, p0, p1, s0, s1, gq_ref, gk_ref, gv_ref, fq_ref, fk_ref, fv_ref, acc):
    k = pl.program_id(1)
    c = sc[1]

    @pl.when(k == 0)
    def _():
        acc[ALL] = jnp.zeros_like(acc)

    r = k // 2
    xr = r ^ sc[2]
    for n, ref in enumerate((h0, h1, h2, h3)):

        @pl.when(xr == n)
        def _():
            h = ref[ALL]
            for t, part in enumerate((p0, p1, s0, s1)):
                acc[:, ROWS * t : ROWS * t + ROWS] += dot_tn(h, part[ALL])

    @pl.when(k == pl.num_programs(1) - 1)
    def _():
        for t in range(POOL):
            cc = c if t < 2 else 1 - c
            g = t % 2
            base = ROWS * t
            qc = pl.ds(pl.multiple_of(cc * ROWS + HD2 * g, HD2), HD2)
            kv = pl.ds(pl.multiple_of(cc * HD2 + HD * g, HD), HD)
            vq = acc[:, base : base + HD2].astype(BF)
            vk = acc[:, base + HD2 : base + HD2 + HD].astype(BF)
            vv = acc[:, base + HD2 + HD : base + ROWS].astype(BF)
            for ref, cols, val in ((gq_ref, qc, vq), (fq_ref, qc, vq), (gk_ref, kv, vk), (fk_ref, kv, vk), (gv_ref, kv, vv), (fv_ref, kv, vv)):
                ref[:, cols] = val


def gqkv_call(sc, hids, parts):
    seq = parts[0].shape[0]
    half = hids[0].shape[1] // 2
    mrow = half // 2

    def hspec(n):
        def im(m, k, p):
            return (jnp.where((k // 2) ^ p[2] == n, k % 2, 0), 2 * p[1] + m)

        return pl.BlockSpec((HD2, mrow), im)

    pspec = pl.BlockSpec((HD2, ROWS), lambda m, k, p: (k, 0))
    outs = [CHIP, ROWS, ROWS]
    return pl.pallas_call(
        gqkv_kernel,
        grid_spec=pltpu.PrefetchScalarGridSpec(
            num_scalar_prefetch=1,
            grid=(2, 8),
            in_specs=[hspec(n) for n in range(POOL)] + [pspec] * POOL,
            out_specs=[pl.BlockSpec((mrow, w), lambda m, k, p: (m, 0)) for w in outs]
            + [pl.BlockSpec((mrow, w), lambda m, k, p: (2 * p[1] + m, 0)) for w in outs],
            scratch_shapes=[pltpu.VMEM((mrow, SEQ), F32)],
        ),
        out_shape=[jax.ShapeDtypeStruct((half, w), BF) for w in outs] + [jax.ShapeDtypeStruct((2 * half, w), BF) for w in outs],
        compiler_params=params(2),
        cost_estimate=cost(2 * seq * half * SEQ, seq * SEQ * POOL + half * SEQ * 2),
        name="grad_wqkv",
    )(sc, *hids, *parts)


def dhid_kernel(sc, p0, p1, s0, s1, wq, wk, wv, xa, xb, dya, dyb, bs, gain, dm_ref, dx_ref, gp_ref, dq_s, dk_s, dv_s, dh_s):
    i = pl.program_id(0)
    nb = pl.num_programs(0) // 2
    own_chip = (i // nb) == sc[0]
    c = sc[1]
    for t, part in enumerate((p0, p1, s0, s1)):
        cc = c if t < 2 else 1 - c
        g = t % 2
        dq_s[:, pl.ds(pl.multiple_of(cc * ROWS + HD2 * g, HD2), HD2)] = part[:, :HD2]
        kv = pl.ds(pl.multiple_of(cc * HD2 + HD * g, HD), HD)
        dk_s[:, kv] = part[:, HD2:HD3]
        dv_s[:, kv] = part[:, HD3:]
    for n in range(5):
        sl = slice(HD2 * n, HD2 * n + HD2)
        acc = dot_nt(dq_s[ALL], wq[sl, :])
        acc = acc + dot_nt(dk_s[ALL], wk[sl, :])
        acc = acc + dot_nt(dv_s[ALL], wv[sl, :])
        dh_s[:, sl] = acc.astype(BF).astype(F32)
    dh = dh_s[ALL]
    x = jnp.where(own_chip, xa[ALL], xb[ALL]).astype(F32)
    rs = lax.rsqrt(jnp.mean(x * x, axis=1, keepdims=YES) + EPS)
    n = x * rs
    g1 = ONE + gain[ALL]
    dhn = dh * n

    @pl.when(i == 0)
    def _():
        gp_ref[ALL] = jnp.zeros_like(gp_ref)

    gp_ref[ALL] += jnp.sum(dhn, axis=0, keepdims=YES)
    mean = jnp.mean(dhn * g1, axis=1, keepdims=YES)
    dx = ((dh * g1 - n * mean) * rs).astype(BF).astype(F32)
    dy = jnp.where(own_chip, dya[ALL], dyb[ALL]).astype(F32)
    dm = (dy + dx).astype(BF)
    dm_ref[ALL] = dm

    @pl.when(own_chip)
    def _():
        dx_ref[ALL] = jnp.where(bs[ALL] >= 0, jnp.zeros_like(dm), dm)


def dhid_call(sc, parts, wq, wk, wv, x_mine, x_peer, dy_mine, dy_peer, bs_col, gain):
    rows, d = x_mine.shape
    rb = HD
    nb = rows // rb

    def prow(i, s):
        return ((i // nb) * 2 + s[1]) * nb + i % nb

    def own(i, s):
        return (jnp.clip(i - nb * s[0], 0, nb - 1), 0)

    def peer(i, s):
        return (jnp.clip(i - nb * (1 - s[0]), 0, nb - 1), 0)

    pspec = pl.BlockSpec((rb, ROWS), lambda i, s: (prow(i, s), 0))
    return pl.pallas_call(
        dhid_kernel,
        grid_spec=pltpu.PrefetchScalarGridSpec(
            num_scalar_prefetch=1,
            grid=(2 * nb,),
            in_specs=[pspec] * POOL
            + [const_spec(wq.shape), const_spec(wk.shape), const_spec(wv.shape)]
            + [pl.BlockSpec((rb, d), own), pl.BlockSpec((rb, d), peer)] * 2
            + [pl.BlockSpec((rb, 1), lambda i, s: (prow(i, s), 0)), const_spec((1, d))],
            out_specs=[
                pl.BlockSpec((rb, d), lambda i, s: (i, 0)),
                pl.BlockSpec((rb, d), own),
                pl.BlockSpec((1, d), lambda i, s: (0, 0)),
            ],
            scratch_shapes=[
                pltpu.VMEM((rb, CHIP), BF),
                pltpu.VMEM((rb, ROWS), BF),
                pltpu.VMEM((rb, ROWS), BF),
                pltpu.VMEM((rb, d), F32),
            ],
        ),
        out_shape=[
            jax.ShapeDtypeStruct((2 * rows, d), BF),
            jax.ShapeDtypeStruct((rows, d), BF),
            jax.ShapeDtypeStruct((1, d), F32),
        ],
        compiler_params=params(1),
        cost_estimate=cost(2 * 2 * rows * d * SEQ, rows * 2 * d * 8 + d * SEQ * 2),
        name="d_hidden",
    )(sc, *parts, wq, wk, wv, x_mine, x_peer, dy_mine, dy_peer, bs_col, gain)


def dsoft_kernel(sc, own_ref, sib_ref, out_ref, buf, sem):
    n = pl.program_id(0)
    c = sc[0]
    last = pl.num_programs(0) - 1

    def copies(im, slot, act):
        for t in range(2):
            b = jnp.minimum(sc[1 + im] + t, 15)
            r = b // POOL
            row = pl.multiple_of(((r // 2) * POOL + b % POOL) * HD, HD)
            dst = buf.at[slot, pl.ds(HD * t, HD), :]
            mine = (r % 2) == c

            @pl.when(mine)
            def _():
                cp = pltpu.make_async_copy(own_ref.at[pl.ds(row, HD), :], dst, sem.at[slot, t])
                cp.start() if act == "start" else cp.wait()

            @pl.when(jnp.logical_not(mine))
            def _():
                cp = pltpu.make_async_copy(sib_ref.at[pl.ds(row, HD), :], dst, sem.at[slot, t])
                cp.start() if act == "start" else cp.wait()

    @pl.when(n == 0)
    def _():
        copies(0, 0, "start")

    @pl.when(n < last)
    def _():
        copies(n + 1, (n + 1) % 2, "start")

    slot = n % 2
    copies(n, slot, "wait")
    off = sc[9 + n]
    row = lax.broadcasted_iota(jnp.int32, (HD, HD2), 0)
    col = lax.broadcasted_iota(jnp.int32, (HD, HD2), 1)
    pick = jnp.where(col == row + off, ONE, 0.0).astype(BF)
    out_ref[ALL] = dot(pick, buf[slot]).astype(BF)


def dsoft_call(sc, dm_own, dm_sib):
    d = dm_own.shape[1]
    return pl.pallas_call(
        dsoft_kernel,
        grid_spec=pltpu.PrefetchScalarGridSpec(
            num_scalar_prefetch=1,
            grid=(8,),
            in_specs=[ANY, ANY],
            out_specs=pl.BlockSpec((HD, d), lambda n, s: (n, 0)),
            scratch_shapes=[pltpu.VMEM((2, HD2, d), BF), pltpu.SemaphoreType.DMA((2, 2))],
        ),
        out_shape=jax.ShapeDtypeStruct((CHIP, d), BF),
        compiler_params=params(1),
        cost_estimate=cost(2 * CHIP * HD2 * d, 3 * CHIP * d * 2),
        name="d_soft",
    )(sc, dm_own, dm_sib)


def dvis_kernel(sc, ds_ref, wp, pooled_ref, gain, out_ref, gp_ref, dp_s):
    i = pl.program_id(0)

    @pl.when(i == 0)
    def _():
        dn = dot_nt(ds_ref[ALL], wp[ALL]).astype(BF).astype(F32)
        pv = pooled_ref[ALL].astype(F32)
        rs = lax.rsqrt(jnp.mean(pv * pv, axis=1, keepdims=YES) + EPS)
        n = pv * rs
        g1 = ONE + gain[ALL]
        dnn = dn * n
        gp_ref[ALL] = jnp.sum(dnn, axis=0, keepdims=YES)
        mean = jnp.mean(dnn * g1, axis=1, keepdims=YES)
        dp_s[ALL] = (((dn * g1 - n * mean) * rs).astype(BF).astype(F32) * (ONE / 16.0)).astype(BF)

    row = lax.broadcasted_iota(jnp.int32, (ROWS, GRID), 0)
    tok = lax.broadcasted_iota(jnp.int32, (ROWS, GRID), 1)
    hit = (tok // SIDE == row // HD) & (tok % SIDE == (row % GRID) // POOL)
    mask = jnp.where(hit, ONE, 0.0).astype(BF)
    out_ref[0] = dot(mask, dp_s[pl.ds(pl.multiple_of(i * GRID, GRID), GRID), :]).astype(BF)


def dvis_call(sc, d_soft, wp, pooled, gain):
    n, dv = pooled.shape
    d = d_soft.shape[1]
    return pl.pallas_call(
        dvis_kernel,
        grid_spec=pltpu.PrefetchScalarGridSpec(
            num_scalar_prefetch=1,
            grid=(n // GRID,),
            in_specs=[
                pl.BlockSpec((n, d), lambda i, s: (s[0], 0), pipeline_mode=pl.Buffered(1)),
                const_spec(wp.shape),
                const_spec(pooled.shape),
                const_spec((1, dv)),
            ],
            out_specs=[pl.BlockSpec((1, ROWS, dv), lambda i, s: (i // POOL, i % POOL, 0)), pl.BlockSpec((1, dv), lambda i, s: (0, 0))],
            scratch_shapes=[pltpu.VMEM((n, dv), BF)],
        ),
        out_shape=[jax.ShapeDtypeStruct((n // BLK, GRID * GRID, dv), BF), jax.ShapeDtypeStruct((1, dv), F32)],
        compiler_params=params(1),
        cost_estimate=cost(2 * n * d * dv + 2 * n * SIDE * HD * dv, n * SIDE * dv * 2 + wp.size * 2),
        name="d_vis",
    )(sc, d_soft, wp, pooled, gain)


def tail_kernel(sc, normed, ds, sq, sk, sv, go_x, go_s, go_d, fq_in, fk_in, fv_in, fo_in, out_ref, fq, fk, fv, fo, sem):
    i = pl.program_id(0)
    row = pl.multiple_of(sc[0] + i * HD, HD)
    orow = jnp.minimum(i, 3) * LANES
    cps = [pltpu.make_async_copy(src, dst.at[pl.ds(row, HD), :], sem.at[n]) for n, (src, dst) in enumerate(((sq, fq), (sk, fk), (sv, fv)))]
    for n, src in enumerate((go_x, go_s, go_d)):
        at = pl.multiple_of(sc[1 + n] + orow, LANES)
        cps.append(pltpu.make_async_copy(src, fo.at[pl.ds(at, LANES), :], sem.at[3 + n]))
    for cp in cps:
        cp.start()
    out_ref[ALL] = dot_tn(normed[ALL], ds[ALL]).astype(BF)
    for cp in cps:
        cp.wait()


def tail_call(sc, normed, ds, halves, quarters, fulls):
    tok, dv = normed.shape
    d = ds.shape[1]
    half = lambda w: pl.BlockSpec((HD, w), lambda i, s: (i, 0))
    quarter = pl.BlockSpec((LANES, d), lambda i, s: (jnp.minimum(i, 3), 0))
    return pl.pallas_call(
        tail_kernel,
        grid_spec=pltpu.PrefetchScalarGridSpec(
            num_scalar_prefetch=1,
            grid=(5,),
            in_specs=[const_spec(normed.shape), pl.BlockSpec((tok, HD2), lambda i, s: (0, i))]
            + [half(h.shape[1]) for h in halves]
            + [quarter] * 3
            + [ANY] * POOL,
            out_specs=[pl.BlockSpec((dv, HD2), lambda i, s: (0, i))] + [ANY] * POOL,
            scratch_shapes=[pltpu.SemaphoreType.DMA((6,))],
        ),
        out_shape=[jax.ShapeDtypeStruct((dv, d), BF)] + [jax.ShapeDtypeStruct(f.shape, BF) for f in fulls],
        input_output_aliases={9 + n: 1 + n for n in range(POOL)},
        compiler_params=params(1),
        cost_estimate=cost(2 * tok * dv * d, tok * (d + dv) * 2 + dv * d * 2),
        name="tail",
    )(sc, normed, ds, *halves, *quarters, *fulls)


def solution(mesh):
    seq_spec = P(('dp', 'cp'))
    part_spec = P('dp')
    rep_spec = P()

    def body(vis, text, img_pos, grad_y, pn_gain, w_proj, pre_gain, w_query, w_key, w_value, q_gain, k_gain, w_out, post_gain):
        rank = lax.axis_index('cp')
        x = rank // 2
        c = rank % 2
        seq = POOL * text.shape[0]
        row_f32 = lambda g: g.astype(F32)[jnp.newaxis, :]
        ints = lambda *v: jnp.stack([jnp.asarray(e, jnp.int32) for e in v])

        pos = img_pos.astype(jnp.int32)
        ids = jnp.arange(8, dtype=jnp.int32)
        start = (jnp.arange(SIDE, dtype=jnp.int32) * HD)[:, jnp.newaxis]
        at_a = (pos[jnp.newaxis] <= start) & (pos[jnp.newaxis] + BLK > start)
        at_b = (pos[jnp.newaxis] > start) & (pos[jnp.newaxis] < start + HD)

        def pick(hit):
            idx = jnp.sum(jnp.where(hit, ids[jnp.newaxis], 0), axis=1)
            shift = jnp.where(jnp.any(hit, axis=1), start[:, 0] - jnp.sum(jnp.where(hit, pos[jnp.newaxis], 0), axis=1), FAR)
            return idx, shift

        ia, da = pick(at_a)
        ib, db = pick(at_b)
        tab = jnp.stack([ia, da, ib, db], axis=1).reshape(-1)
        rows = jnp.arange(seq, dtype=jnp.int32)
        inside = (rows[:, jnp.newaxis] >= pos[jnp.newaxis]) & (rows[:, jnp.newaxis] < pos[jnp.newaxis] + BLK)
        blk_start = jnp.where(jnp.any(inside, axis=1), jnp.sum(jnp.where(inside, pos[jnp.newaxis], 0), axis=1), -FAR)
        bs_col = blk_start[:, jnp.newaxis]
        bs_row = blk_start.reshape(seq // QB, 1, QB)
        qb_lo = jnp.arange(seq // QB, dtype=jnp.int32) * QB
        cross = (pos[jnp.newaxis] < (qb_lo + QB)[:, jnp.newaxis]) & (pos[jnp.newaxis] + BLK > (qb_lo + QB)[:, jnp.newaxis])
        cross = jnp.any(cross, axis=1).astype(jnp.int32)
        nblk = jnp.arange(seq // QB, dtype=jnp.int32)
        nkv = nblk + 1 + cross
        first_q = nblk - jnp.concatenate([jnp.zeros((1,), jnp.int32), cross[:-1]])

        def swap(a, perm):
            return lax.ppermute(a, 'cp', perm)

        pooled, normed = pool_call(vis, row_f32(pn_gain))
        normed_x = swap(normed, XPERM)
        text_x = swap(text, XPERM)
        dy_x = swap(grad_y, XPERM)
        theirs = swap(jnp.stack([normed, normed_x]), SPERM)
        normed_all = jnp.zeros((POOL,) + normed.shape, BF)
        for piece, slot in ((normed, 0), (normed_x, 2), (theirs[0], 1), (theirs[1], 3)):
            normed_all = lax.dynamic_update_index_in_dim(normed_all, piece, rank ^ slot, 0)
        normed_all = normed_all.reshape(-1, normed.shape[1])
        soft = jnp.dot(normed_all, w_proj, preferred_element_type=F32).astype(BF)

        pre = row_f32(pre_gain)
        qg, kg = row_f32(q_gain), row_f32(k_gain)
        x_mine, h_mine = merge_call(tab, ints(rank), soft, text, pre)
        h_sib = swap(h_mine, SPERM)
        inv_freq = ROPE_BASE ** (-jnp.arange(0, HD, 2).astype(F32) / HD)
        angle = (rows.astype(F32) / ROPE_SCALE)[:, jnp.newaxis] * inv_freq[jnp.newaxis, :]
        cos, sin = jnp.cos(angle), jnp.sin(angle)
        qkv_args = (w_query, w_key, w_value, qg, kg, cos, sin)
        bufs = qkv_call(ints(x, c), h_mine, h_sib, *qkv_args, ())
        x_peer, h_peer = merge_call(tab, ints(rank ^ 2), soft, text_x, pre)
        h_diag = swap(h_peer, SPERM)
        q0, q1, qr0, qr1, k0, k1, kr0, kr1, v0, v1 = qkv_call(ints(1 - x, c), h_peer, h_diag, *qkv_args, bufs)

        o0, lse0 = fwd_call(nkv, q0, k0, v0, bs_col)
        o0s = swap(o0, SPERM)
        o1, lse1 = fwd_call(nkv, q1, k1, v1, bs_col)
        o1s = swap(o1, SPERM)

        post = row_f32(post_gain)
        y, dp_m, dam0, dam1, das0, das1, gpost_m = out_call(ints(x, c), (o0, o1), (o0s, o1s), w_out, grad_y, post, (x_mine,))
        das0, das1 = swap(das0, SPERM), swap(das1, SPERM)
        dp_sm = swap(dp_m, SPERM)
        dp_p, dap0, dap1, dbs0, dbs1, gpost_p = out_call(ints(1 - x, c), (o0, o1), (o0s, o1s), w_out, dy_x, post)
        dbs0, dbs1 = swap(dbs0, SPERM), swap(dbs1, SPERM)
        dp_sp = swap(dp_p, SPERM)

        bsc = jnp.concatenate([ints(rank), first_q])
        bwd_args = (cos, sin, qg, kg)
        part0, gq0, gk0 = bwd_call(bsc, q0, (dam0, dap0, das0, dbs0), o0, k0, v0, lse0, bs_row, qr0, kr0, *bwd_args)
        part0s = swap(part0, SPERM)
        part1, gq1, gk1 = bwd_call(bsc, q1, (dam1, dap1, das1, dbs1), o1, k1, v1, lse1, bs_row, qr1, kr1, *bwd_args)
        part1s = swap(part1, SPERM)

        go, go_full = gwo_call(ints(x, c, rank, *[rank ^ n for n in SLOT]), o0, o1, (dp_m, dp_p, dp_sm, dp_sp))
        go_x = swap(go, XPERM)
        go_s = swap(go, SPERM)
        early = jnp.concatenate([gq0 + gq1, gk0 + gk1, gpost_m + gpost_p], axis=1)
        early = early + swap(early, SPERM)

        parts = (part0, part1, part0s, part1s)
        dm, grad_text, gpre = dhid_call(ints(x, c), parts, w_query, w_key, w_value, x_mine, x_peer, grad_y, dy_x, bs_col, pre)
        dm_s = swap(dm, SPERM)
        gpre = gpre + swap(gpre, SPERM)
        go_d = swap(go_x, SPERM)
        *g_half, fq, fk, fv = gqkv_call(ints(x, c, rank), (h_mine, h_sib, h_peer, h_diag), parts)
        halves = [swap(a, SPERM) for a in g_half]
        d_soft = dsoft_call(jnp.concatenate([ints(c), pos // HD, pos % HD]), dm, dm_s)
        grad_vis, gpn = dvis_call(ints(rank), d_soft, w_proj, pooled, row_f32(pn_gain))
        gpn = gpn + swap(gpn, XPERM)
        gpn = gpn + swap(gpn, SPERM)
        where = ints((1 - c) * w_query.shape[0] // 2, (2 * c + 1 - x) * HD2, (2 - 2 * c + x) * HD2, (3 - 2 * c - x) * HD2)
        g_proj, gq, gk, gv, g_out = tail_call(where, normed_all, d_soft, halves, (go_x, go_s, go_d), (fq, fk, fv, go_full))

        early = early[0].astype(BF)
        sq, sk, spost = early[:HD], early[HD:HD2], early[HD2:]
        return (y, grad_text, grad_vis, gpn[0].astype(BF), g_proj, gpre[0].astype(BF), gq, gk, gv, sq, sk, g_out, spost)

    in_specs = (seq_spec, seq_spec, part_spec, seq_spec) + (rep_spec,) * NBUF
    out_specs = (seq_spec, seq_spec, seq_spec) + (part_spec,) * NBUF
    return jax.shard_map(body, mesh=mesh, in_specs=in_specs, out_specs=out_specs, check_vma=False)
```

profile of v0, /device:TPU:0, one launch (start us, length us, event | category | flops | bytes accessed | tf_op | source)
XLA Modules:
  0.0 876.9 jit_solution(11479038966061078118)
XLA Ops:
  0.6 1.3 reshape.136.gain_ref.gain
  1.9 11.4 %pool.1 = (bf16[512,1152]{1,0:T(8,128)(2,1)}, bf16[512,1152]{1,0:T(8,128)(2,1)}) custom-call(bf16[2,4096,1152]{2,1,0:T(8,128)(2,1)} %vis_ref.1, f32[1,1152]{1,0:T(1,128)} %reshape.136.gain_ref.gain), custom_call_target="tpu_custom_call" | custom-call | flops 1207959552 | bytes 18874368 | tf_op jit(solution)/shard_map/pool/pallas_call | solution.py:85
  13.4 3.3 collective-permute-start
  16.7 26.2 %collective-permute-done = bf16[512,1152]{1,0:T(8,128)(2,1)S(1)} collective-permute-done((bf16[512,1152]{1,0:T(8,128)(2,1)}, bf16[512,1152]{1,0:T(8,128)(2,1)S(1)}, u32[]{:S(2)}, u32[]{:S(2)}) %collective-permute-start) | collective-permute-done | bytes 1179680 | tf_op jit(solution)/shard_map/ppermute | solution.py:872
  42.9 3.0 pad_maximum_fusion
  45.9 1.7 collective-permute-start.2
  47.6 0.6 and_select_fusion.1
  48.5 0.6 reshape.134.tab
  49.1 0.6 reshape.137.gain
  50.7 1.4 slice_dynamic-update-slice_fusion.1
  52.2 1.4 slice_dynamic-update-slice_fusion
  53.7 20.4 %convolution_convert_fusion.soft = bf16[2048,2560]{1,0:T(8,128)(2,1)} fusion(bf16[2048,1152]{1,0:T(8,128)(2,1)S(1)} %bitcast.37, bf16[1152,2560]{1,0:T(8,128)(2,1)} %wp.1), kind=kOutput, calls=%fused_computation | convolution fusion | flops 12084838400 | bytes 21102592 | tf_op jit(solution)/shard_map/dot_general | solution.py:883
  74.0 11.7 %merge.3 = (bf16[1024,2560]{1,0:T(8,128)(2,1)}, bf16[1024,2560]{1,0:T(8,128)(2,1)}) custom-call(s32[64]{0:T(128)} %reshape.134.tab, s32[1]{0:T(128)} %bitcast.15.sc, bf16[2048,2560]{1,0:T(8,128)(2,1)} %convolution_convert_fusion.soft, bf16[1024,2560]{1,0:T(8,128)(2,1)} %text.1, f32[1,2560]{1,0:T(1,128)} %reshape.137.gain), custom_call_target="tpu_custom_call" | custom-call | flops 2684354560 | bytes 26214400 | tf_op jit(solution)/shard_map/merge/pallas_call | solution.py:128
  85.7 1.2 collective-permute-start.4
  86.9 74.7 %collective-permute-done.2.text = bf16[1024,2560]{1,0:T(8,128)(2,1)} collective-permute-done((bf16[1024,2560]{1,0:T(8,128)(2,1)}, bf16[1024,2560]{1,0:T(8,128)(2,1)}, u32[]{:S(2)}, u32[]{:S(2)}) %collective-permute-start.2) | collective-permute-done | bytes 5242912 | tf_op jit(solution)/shard_map/ppermute | solution.py:872
  161.6 12.9 %merge.2 = (bf16[1024,2560]{1,0:T(8,128)(2,1)}, bf16[1024,2560]{1,0:T(8,128)(2,1)}) custom-call(s32[64]{0:T(128)} %reshape.134.tab, s32[1]{0:T(128)} %bitcast.9.sc, bf16[2048,2560]{1,0:T(8,128)(2,1)} %convolution_convert_fusion.soft, bf16[1024,2560]{1,0:T(8,128)(2,1)} %collective-permute-done.2.text, f32[1,2560]{1,0:T(1,128)} %reshape.137.gain), custom_call_target="tpu_custom_call" | custom-call | flops 2684354560 | bytes 26214400 | tf_op jit(solution)/shard_map/merge/pallas_call | solution.py:128
  174.5 1.4 collective-permute-start.7
  175.9 0.6 broadcast_in_dim.125
  176.5 0.6 broadcast_in_dim.126
  177.3 2.0 copy.47.bs_ref.bs
  179.3 0.6 pad_add_fusion.1.sc
  180.0 0.6 pad_add_fusion.2.sc
  180.7 0.5 add_add_fusion.nkv
  181.2 9.3 %multiply_sine_fusion = (f32[4096,128]{1,0:T(8,128)}, f32[4096,128]{1,0:T(8,128)}) fusion(f32[128]{0:T(128)S(1)} %multiply_power_fusion, f32[4096]{0:T(1024)S(1)} %convert_multiply_fusion), kind=kLoop, calls=%fused_computation.1 | loop fusion | flops 524288 | bytes 4211200 | tf_op jit(solution)/shard_map/sin | solution.py:891
  190.5 32.8 %qkv.2 = (bf16[4096,512]{1,0:T(8,128)(2,1)}, bf16[4096,512]{1,0:T(8,128)(2,1)}, bf16[4096,512]{1,0:T(8,128)(2,1)}, bf16[4096,512]{1,0:T(8,128)(2,1)}, bf16[4096,...) custom-call(s32[2]{0:T(128)} %pad_add_fusion.1.sc, ...), custom_call_target="tpu_custom_call" | custom-call | flops 21474836480 | bytes 35651584 | tf_op jit(solution)/shard_map/qkv/pallas_call | solution.py:197
  223.3 32.8 %qkv.3 = (bf16[4096,512]{1,0:T(8,128)(2,1)}, bf16[4096,512]{1,0:T(8,128)(2,1)}, bf16[4096,512]{1,0:T(8,128)(2,1)}, bf16[4096,512]{1,0:T(8,128)(2,1)}, bf16[4096,...) custom-call(s32[2]{0:T(128)} %pad_add_fusion.2.sc, ...), custom_call_target="tpu_custom_call", output_to_operand_aliasing={{0}: (10, {}), {1}: (11, {}), {2}: (12, {}), {3}: (13, {}),... | custom-call | flops 21474836480 | bytes 35651584 | tf_op jit(solution)/shard_map/qkv/pallas_call | solution.py:197
  256.2 48.7 %attn_fwd.3 = (bf16[4096,512]{1,0:T(8,128)(2,1)}, f32[8,2,512]{2,1,0:T(2,128)}) custom-call(s32[8]{0:T(128)} %add_add_fusion.nkv, bf16[4096,512]{1,0:T(8,128)(2,1)} %get-tuple-element.97.q_ref, bf16[4096,256]{1,0:T(8,128)(2,1)} %get-tuple-element.98.k_ref, bf16[4096,256]{1,0:T(8,128)(2,1)} %get-tuple-element.99.v_ref, s32[4096,1]{1,0:T(8,128)} %copy.47.bs_ref.bs), custom_call_target="tpu_custom_call" | custom-call | flops 24051816448 | bytes 12582912 | tf_op jit(solution)/shard_map/attn_fwd/pallas_call | solution.py:264
  304.9 48.6 %attn_fwd.2 = (bf16[4096,512]{1,0:T(8,128)(2,1)}, f32[8,2,512]{2,1,0:T(2,128)}) custom-call(s32[8]{0:T(128)} %add_add_fusion.nkv, bf16[4096,512]{1,0:T(8,128)(2,1)} %get-tuple-element.93.q_ref, bf16[4096,256]{1,0:T(8,128)(2,1)} %get-tuple-element.94.k_ref, bf16[4096,256]{1,0:T(8,128)(2,1)} %get-tuple-element.95.v_ref, s32[4096,1]{1,0:T(8,128)} %copy.47.bs_ref.bs), custom_call_target="tpu_custom_call" | custom-call | flops 24051816448 | bytes 12582912 | tf_op jit(solution)/shard_map/attn_fwd/pallas_call | solution.py:264
  353.4 0.5 collective-permute-start.5
  353.9 0.6 reshape.140.gain
  354.6 6.5 collective-permute-done.5.os0
  361.1 33.6 %out_proj.3 = (bf16[1024,2560]{1,0:T(8,128)(2,1)}, bf16[1024,512]{1,0:T(8,128)(2,1)}, bf16[1024,512]{1,0:T(8,128)(2,1)}, bf16[1024,512]{1,0:T(8,128)(2,1)}, bf16...) custom-call(s32[2]{0:T(128)} %pad_add_fusion.2.sc, bf16[4096,512]{1,0:T(8,128)(2,1)} %get-tuple-element.96.oo0.o_ref.o0, ...), custom_call_target="tpu_custom_call" | custom-call | flops 21474836480 | bytes 36700160 | tf_op jit(solution)/shard_map/out_proj/pallas_call | solution.py:330
  395.0 35.4 %out_proj.2 = (bf16[1024,2560]{1,0:T(8,128)(2,1)}, bf16[1024,2560]{1,0:T(8,128)(2,1)}, bf16[1024,512]{1,0:T(8,128)(2,1)}, bf16[1024,512]{1,0:T(8,128)(2,1)}, bf1...) custom-call(s32[2]{0:T(128)} %pad_add_fusion.1.sc, ...), custom_call_target="tpu_custom_call" | custom-call | flops 21474836480 | bytes 36700160 | tf_op jit(solution)/shard_map/out_proj/pallas_call | solution.py:330
  430.6 0.6 pad_add_fusion.3.sc
  431.7 1.7 collective-permute-done.10.do_c
  433.4 91.0 %attn_bwd.3 = (bf16[4096,1024]{1,0:T(8,128)(2,1)}, f32[1,256]{1,0:T(1,128)}, f32[1,256]{1,0:T(1,128)}) custom-call(s32[9]{0:T(128)} %pad_add_fusion.3.sc, bf16[4096,512]{1,0:T(8,128)(2,1)} %get-tuple-element.97.q_ref, bf16[1024,512]{1,0:T(8,128)(2,1)} %get-tuple-element.111.do_a, bf16[1024,512]{1,0:T(8,128)(2,1)} %get-tuple-element.112.do_b, ...), custom_call_target="tpu_custom_call" | custom-call | flops 51539607552 | bytes 32768000 | tf_op jit(solution)/shard_map/attn_bwd/pallas_call | solution.py:448
  524.6 1.0 copy-done.15
  525.5 90.5 %attn_bwd.2 = (bf16[4096,1024]{1,0:T(8,128)(2,1)}, f32[1,256]{1,0:T(1,128)}, f32[1,256]{1,0:T(1,128)}) custom-call(s32[9]{0:T(128)} %pad_add_fusion.3.sc, bf16[4096,512]{1,0:T(8,128)(2,1)} %get-tuple-element.93.q_ref, bf16[1024,512]{1,0:T(8,128)(2,1)} %get-tuple-element.103.do_a, bf16[1024,512]{1,0:T(8,128)(2,1)} %get-tuple-element.104.do_b, ...), custom_call_target="tpu_custom_call" | custom-call | flops 51539607552 | bytes 32768000 | tf_op jit(solution)/shard_map/attn_bwd/pallas_call | solution.py:448
  616.0 0.4 collective-permute-start.12
  616.9 12.6 %collective-permute-done.12.s0 = bf16[4096,1024]{1,0:T(8,128)(2,1)} collective-permute-done((bf16[4096,1024]{1,0:T(8,128)(2,1)}, bf16[4096,1024]{1,0:T(8,128)(2,1)}, u32[]{:S(2)}, u32[]{:S(2)}) %collective-permute-start.12) | collective-permute-done | bytes 8388640 | tf_op jit(solution)/shard_map/ppermute | solution.py:872
  629.5 76.6 %d_hidden.1 = (bf16[2048,2560]{1,0:T(8,128)(2,1)}, bf16[1024,2560]{1,0:T(8,128)(2,1)}, f32[1,2560]{1,0:T(1,128)}) custom-call(s32[2]{0:T(128)} %pad_add_fusion.1.sc, bf16[4096,1024]{1,0:T(8,128)(2,1)} %get-tuple-element.110.p0, bf16[4096,1024]{1,0:T(8,128)(2,1)} %get-tuple-element.118.p1, bf16[4096,1024]{1,0:T(8,128)(2,1)} %collective-permute-done.12.s0, ...), custom_call_target="tpu_custom_call" | custom-call | flops 42949672960 | bytes 62914560 | tf_op jit(solution)/shard_map/d_hidden/pallas_call | solution.py:656
  706.1 0.5 collective-permute-start.14
  706.6 0.6 stack.104.sc
  707.2 0.6 pad_add_fusion.6.sc
  707.8 23.1 %grad_wo.1 = (bf16[512,2560]{1,0:T(8,128)(2,1)}, bf16[2048,2560]{1,0:T(8,128)(2,1)}) custom-call(s32[7]{0:T(128)} %stack.104.sc, bf16[4096,512]{1,0:T(8,128)(2,1)} %get-tuple-element.96.oo0.o_ref.o0, bf16[4096,512]{1,0:T(8,128)(2,1)} %get-tuple-element.100.oo1.o_ref.o1, bf16[1024,2560]{1,0:T(8,128)(2,1)} %get-tuple-element.128.dp0, ...), custom_call_target="tpu_custom_call" | custom-call | flops 10737418240 | bytes 29360128 | tf_op jit(solution)/shard_map/grad_wo/pallas_call | solution.py:521
  731.0 0.6 collective-permute-start.22
  731.6 63.8 %grad_wqkv.1 = (bf16[1280,2048]{1,0:T(8,128)(2,1)}, bf16[1280,1024]{1,0:T(8,128)(2,1)}, bf16[1280,1024]{1,0:T(8,128)(2,1)}, bf16[2560,2048]{1,0:T(8,128)(2,1)}, ...) custom-call(s32[3]{0:T(128)} %pad_add_fusion.6.sc, bf16[1024,2560]{1,0:T(8,128)(2,1)} %get-tuple-element.82.ha.h0, ...), custom_call_target="tpu_custom_call" | custom-call | flops 42949672960 | bytes 77594624 | tf_op jit(solution)/shard_map/grad_wqkv/pallas_call | solution.py:583
  795.5 0.6 pad_add_fusion.4.sc
  796.2 0.5 collective-permute-start.26
  796.8 15.9 %d_soft.1.ds_ref.ds = bf16[2048,2560]{1,0:T(8,128)(2,1)} custom-call(s32[17]{0:T(128)} %pad_add_fusion.4.sc, bf16[2048,2560]{1,0:T(8,128)(2,1)} %get-tuple-element.121.own_ref, bf16[2048,2560]{1,0:T(8,128)(2,1)} %collective-permute-done.14.sib_ref), custom_call_target="tpu_custom_call" | custom-call | flops 5368709120 | bytes 31457280 | tf_op jit(solution)/shard_map/d_soft/pallas_call | solution.py:730
  812.7 17.9 %d_vis.1 = (bf16[2,4096,1152]{2,1,0:T(8,128)(2,1)}, f32[1,1152]{1,0:T(1,128)}) custom-call(s32[1]{0:T(128)} %bitcast.15.sc, bf16[2048,2560]{1,0:T(8,128)(2,1)} %d_soft.1.ds_ref.ds, bf16[1152,2560]{1,0:T(8,128)(2,1)} %wp.1, bf16[512,1152]{1,0:T(8,128)(2,1)} %get-tuple-element.122.pooled_ref, f32[1,1152]{1,0:T(1,128)} %reshape.136.gain_ref.gain), custom_call_target="tpu_custom_call" | custom-call | flops 7851737088 | bytes 24772608 | tf_op jit(solution)/shard_map/d_vis/pallas_call | solution.py:771
  830.6 1.4 collective-permute-start.15
  832.6 1.8 collective-permute-done.15
  834.4 0.6 pad_add_fusion.5.sc
  835.0 0.5 slice_reduce_fusion.1
  835.6 0.6 slice_reduce_fusion
  836.2 0.6 convert_reduce_fusion
  836.8 0.7 add.94
  837.5 0.5 collective-permute-start.16
  838.1 2.9 collective-permute-done.24.go_d
  841.0 3.7 collective-permute-done.18.sk
  844.7 3.7 collective-permute-done.19.sv
  848.5 27.6 %tail.1 = (bf16[1152,2560]{1,0:T(8,128)(2,1)}, bf16[2560,2048]{1,0:T(8,128)(2,1)}, bf16[2560,1024]{1,0:T(8,128)(2,1)}, bf16[2560,1024]{1,0:T(8,128)(2,1)}, bf16[2048,2560]{1,0:T(8,128)(2,1)}) custom-call(s32[4]{0:T(128)} %pad_add_fusion.5.sc, ...), custom_call_target="tpu_custom_call", output_to_operand_aliasing={{1}: (9, {}), {2}: (10, {}), {3}: (11, {}), {4}: (12, {})} | custom-call | flops 12079595520 | bytes 21102592 | tf_op jit(solution)/shard_map/tail/pallas_call | solution.py:812
  876.1 0.6 convert_reduce_fusion.1
  (92 shorter events, 4.5 us)
Async XLA Ops:
  13.4 34.3 %copy-start.3 = (s32[8]{0:T(128)S(1)}, s32[8]{0:T(128)}, u32[]{:S(2)}) copy-start(s32[8]{0:T(128)} %param.16) | copy-start | bytes 100
  13.4 35.8 %copy-start.7 = (bf16[2560]{0:T(1024)(128)(2,1)S(1)}, bf16[2560]{0:T(1024)(128)(2,1)}, u32[]{:S(2)}) copy-start(bf16[2560]{0:T(1024)(128)(2,1)} %param.20) | copy-start | bytes 15364
  13.4 29.5 %collective-permute-start = (bf16[512,1152]{1,0:T(8,128)(2,1)}, bf16[512,1152]{1,0:T(8,128)(2,1)S(1)}, u32[]{:S(2)}, u32[]{:S(2)}) collective-permute-start(bf16[512,1152]{1,0:T(8,128)(2,1)} %get-tuple-element.80), channel_id=1, source_target_pairs={{0,2},{2,0},{1,3},{3,1},{4,6},{6,4},{5,7},{7,5}} | collective-permute-start | bytes 3538952 | tf_op jit(solution)/shard_map/ppermute | solution.py:872
  42.9 7.2 copy-start.1
  45.9 4.9 collective-permute-start.1
  45.9 115.8 %collective-permute-start.2 = (bf16[1024,2560]{1,0:T(8,128)(2,1)}, bf16[1024,2560]{1,0:T(8,128)(2,1)}, u32[]{:S(2)}, u32[]{:S(2)}) collective-permute-start(bf16[1024,2560]{1,0:T(8,128)(2,1)} %text.1), channel_id=1, source_target_pairs={{0,2},{2,0},{1,3},{3,1},{4,6},{6,4},{5,7},{7,5}} | collective-permute-start | bytes 15728648 | tf_op jit(solution)/shard_map/ppermute | solution.py:872
  53.6 20.4 %copy-start = (bf16[4,512,1152]{2,1,0:T(8,128)(2,1)}, bf16[4,512,1152]{2,1,0:T(8,128)(2,1)S(1)}, u32[]{:S(2)}) copy-start(bf16[4,512,1152]{2,1,0:T(8,128)(2,1)S(1)} %slice_dynamic-update-slice_fusion) | copy-start | bytes 14155780
  85.7 104.8 %collective-permute-start.4 = (bf16[1024,2560]{1,0:T(8,128)(2,1)}, bf16[1024,2560]{1,0:T(8,128)(2,1)}, u32[]{:S(2)}, u32[]{:S(2)}) collective-permute-start(bf16[1024,2560]{1,0:T(8,128)(2,1)} %get-tuple-element.82.ha.h0), channel_id=1, source_target_pairs={{0,1},{1,0},{2,3},{3,2},{4,5},{5,4},{6,7},{7,6}} | collective-permute-start | bytes 15728648 | tf_op jit(solution)/shard_map/ppermute | solution.py:872
  161.6 14.3 %copy-start.16 = (bf16[256]{0:T(256)(128)(2,1)S(1)}, bf16[256]{0:T(256)(128)(2,1)}, u32[]{:S(2)}) copy-start(bf16[256]{0:T(256)(128)(2,1)} %param.24) | copy-start | bytes 1540
  161.6 14.9 %copy-start.17 = (bf16[256]{0:T(256)(128)(2,1)S(1)}, bf16[256]{0:T(256)(128)(2,1)}, u32[]{:S(2)}) copy-start(bf16[256]{0:T(256)(128)(2,1)} %param.25) | copy-start | bytes 1540
  174.5 48.8 %collective-permute-start.3 = (bf16[1024,2560]{1,0:T(8,128)(2,1)}, bf16[1024,2560]{1,0:T(8,128)(2,1)}, u32[]{:S(2)}, u32[]{:S(2)}) collective-permute-start(bf16[1024,2560]{1,0:T(8,128)(2,1)} %get-tuple-element.81.ha.h2), channel_id=1, source_target_pairs={{0,1},{1,0},{2,3},{3,2},{4,5},{5,4},{6,7},{7,6}} | collective-permute-start | bytes 15728648 | tf_op jit(solution)/shard_map/ppermute | solution.py:872
  174.5 180.0 %collective-permute-start.7 = (bf16[1024,2560]{1,0:T(8,128)(2,1)}, bf16[1024,2560]{1,0:T(8,128)(2,1)}, u32[]{:S(2)}, u32[]{:S(2)}) collective-permute-start(bf16[1024,2560]{1,0:T(8,128)(2,1)} %dya.1), channel_id=1, source_target_pairs={{0,2},{2,0},{1,3},{3,1},{4,6},{6,4},{5,7},{7,5}} | collective-permute-start | bytes 15728648 | tf_op jit(solution)/shard_map/ppermute | solution.py:872
  177.3 46.0 %copy-start.2 = (s32[4096]{0:T(1024)}, s32[4096]{0:T(1024)S(1)}, u32[]{:S(2)}) copy-start(s32[4096]{0:T(1024)S(1)} %broadcast_select_fusion) | copy-start | bytes 49156
  304.8 49.7 %collective-permute-start.6 = (bf16[4096,512]{1,0:T(8,128)(2,1)}, bf16[4096,512]{1,0:T(8,128)(2,1)}, u32[]{:S(2)}, u32[]{:S(2)}) collective-permute-start(bf16[4096,512]{1,0:T(8,128)(2,1)} %get-tuple-element.100.oo1.o_ref.o1), channel_id=1, source_target_pairs={{0,1},{1,0},{2,3},{3,2},{4,5},{5,4},{6,7},{7,6}} | collective-permute-start | bytes 12582920 | tf_op jit(solution)/shard_map/ppermute | solution.py:872
  304.8 49.1 %copy-start.8 = (bf16[2560]{0:T(1024)(128)(2,1)S(1)}, bf16[2560]{0:T(1024)(128)(2,1)}, u32[]{:S(2)}) copy-start(bf16[2560]{0:T(1024)(128)(2,1)} %param.27) | copy-start | bytes 15364
  353.4 7.6 collective-permute-start.5
  394.7 37.1 %collective-permute-start.11 = (bf16[1024,512]{1,0:T(8,128)(2,1)}, bf16[1024,512]{1,0:T(8,128)(2,1)}, u32[]{:S(2)}, u32[]{:S(2)}) collective-permute-start(bf16[1024,512]{1,0:T(8,128)(2,1)} %get-tuple-element.114), channel_id=1, source_target_pairs={{0,1},{1,0},{2,3},{3,2},{4,5},{5,4},{6,7},{7,6}} | collective-permute-start | bytes 3145736 | tf_op jit(solution)/shard_map/ppermute | solution.py:872
  430.4 3.0 collective-permute-start.10
  431.2 93.3 %collective-permute-start.9 = (bf16[1024,512]{1,0:T(8,128)(2,1)}, bf16[1024,512]{1,0:T(8,128)(2,1)S(1)}, u32[]{:S(2)}, u32[]{:S(2)}) collective-permute-start(bf16[1024,512]{1,0:T(8,128)(2,1)} %get-tuple-element.106), channel_id=1, source_target_pairs={{0,1},{1,0},{2,3},{3,2},{4,5},{5,4},{6,7},{7,6}} | collective-permute-start | bytes 3145736 | tf_op jit(solution)/shard_map/ppermute | solution.py:872
  431.6 93.0 %collective-permute-start.8 = (bf16[1024,512]{1,0:T(8,128)(2,1)}, bf16[1024,512]{1,0:T(8,128)(2,1)}, u32[]{:S(2)}, u32[]{:S(2)}) collective-permute-start(bf16[1024,512]{1,0:T(8,128)(2,1)} %get-tuple-element.105), channel_id=1, source_target_pairs={{0,1},{1,0},{2,3},{3,2},{4,5},{5,4},{6,7},{7,6}} | collective-permute-start | bytes 3145736 | tf_op jit(solution)/shard_map/ppermute | solution.py:872
  524.4 92.5 %collective-permute-start.13 = (bf16[4096,1024]{1,0:T(8,128)(2,1)}, bf16[4096,1024]{1,0:T(8,128)(2,1)}, u32[]{:S(2)}, u32[]{:S(2)}) collective-permute-start(bf16[4096,1024]{1,0:T(8,128)(2,1)} %get-tuple-element.118.p1), channel_id=1, source_target_pairs={{0,1},{1,0},{2,3},{3,2},{4,5},{5,4},{6,7},{7,6}} | collective-permute-start | bytes 25165832 | tf_op jit(solution)/shard_map/ppermute | solution.py:872
  524.6 1.0 copy-start.15
  616.0 13.5 %collective-permute-start.12 = (bf16[4096,1024]{1,0:T(8,128)(2,1)}, bf16[4096,1024]{1,0:T(8,128)(2,1)}, u32[]{:S(2)}, u32[]{:S(2)}) collective-permute-start(bf16[4096,1024]{1,0:T(8,128)(2,1)} %get-tuple-element.110.p0), channel_id=1, source_target_pairs={{0,1},{1,0},{2,3},{3,2},{4,5},{5,4},{6,7},{7,6}} | collective-permute-start | bytes 25165832 | tf_op jit(solution)/shard_map/ppermute | solution.py:872
  616.4 91.4 %collective-permute-start.21 = (bf16[1024,2560]{1,0:T(8,128)(2,1)}, bf16[1024,2560]{1,0:T(8,128)(2,1)}, u32[]{:S(2)}, u32[]{:S(2)}) collective-permute-start(bf16[1024,2560]{1,0:T(8,128)(2,1)} %get-tuple-element.129.dp1), channel_id=1, source_target_pairs={{0,1},{1,0},{2,3},{3,2},{4,5},{5,4},{6,7},{7,6}} | collective-permute-start | bytes 15728648 | tf_op jit(solution)/shard_map/ppermute | solution.py:872
  616.6 91.2 %collective-permute-start.20 = (bf16[1024,2560]{1,0:T(8,128)(2,1)}, bf16[1024,2560]{1,0:T(8,128)(2,1)}, u32[]{:S(2)}, u32[]{:S(2)}) collective-permute-start(bf16[1024,2560]{1,0:T(8,128)(2,1)} %get-tuple-element.128.dp0), channel_id=1, source_target_pairs={{0,1},{1,0},{2,3},{3,2},{4,5},{5,4},{6,7},{7,6}} | collective-permute-start | bytes 15728648 | tf_op jit(solution)/shard_map/ppermute | solution.py:872
  706.1 90.6 %collective-permute-start.14 = (bf16[2048,2560]{1,0:T(8,128)(2,1)}, bf16[2048,2560]{1,0:T(8,128)(2,1)}, u32[]{:S(2)}, u32[]{:S(2)}) collective-permute-start(bf16[2048,2560]{1,0:T(8,128)(2,1)} %get-tuple-element.121.own_ref), channel_id=1, source_target_pairs={{0,1},{1,0},{2,3},{3,2},{4,5},{5,4},{6,7},{7,6}} | collective-permute-start | bytes 31457288 | tf_op jit(solution)/shard_map/ppermute | solution.py:872
  730.9 64.6 %copy-start.9 = (s32[8]{0:T(128)S(1)}, s32[8]{0:T(128)}, u32[]{:S(2)}) copy-start(s32[8]{0:T(128)} %get-tuple-element.159) | copy-start | bytes 100
  730.9 64.6 %copy-start.10 = (s32[8]{0:T(128)S(1)}, s32[8]{0:T(128)}, u32[]{:S(2)}) copy-start(s32[8]{0:T(128)} %get-tuple-element.160) | copy-start | bytes 100
  730.9 65.2 %copy-start.5 = (f32[1,2560]{1,0:T(1,128)S(1)}, f32[1,2560]{1,0:T(1,128)}, u32[]{:S(2)}) copy-start(f32[1,2560]{1,0:T(1,128)} %get-tuple-element.145) | copy-start | bytes 30724
  730.9 65.2 %copy-start.6 = (f32[1,2560]{1,0:T(1,128)S(1)}, f32[1,2560]{1,0:T(1,128)}, u32[]{:S(2)}) copy-start(f32[1,2560]{1,0:T(1,128)} %get-tuple-element.144) | copy-start | bytes 30724
  730.9 65.2 %copy-start.12 = (f32[1,256]{1,0:T(1,128)S(1)}, f32[1,256]{1,0:T(1,128)}, u32[]{:S(2)}) copy-start(f32[1,256]{1,0:T(1,128)} %get-tuple-element.141) | copy-start | bytes 3076
  731.0 65.2 %copy-start.14 = (f32[1,256]{1,0:T(1,128)S(1)}, f32[1,256]{1,0:T(1,128)}, u32[]{:S(2)}) copy-start(f32[1,256]{1,0:T(1,128)} %get-tuple-element.140) | copy-start | bytes 3076
  731.0 65.2 %copy-start.11 = (f32[1,256]{1,0:T(1,128)S(1)}, f32[1,256]{1,0:T(1,128)}, u32[]{:S(2)}) copy-start(f32[1,256]{1,0:T(1,128)} %get-tuple-element.143) | copy-start | bytes 3076
  731.0 65.2 %copy-start.13 = (f32[1,256]{1,0:T(1,128)S(1)}, f32[1,256]{1,0:T(1,128)}, u32[]{:S(2)}) copy-start(f32[1,256]{1,0:T(1,128)} %get-tuple-element.142) | copy-start | bytes 3076
  731.0 65.7 %copy-start.4 = (f32[1,2560]{1,0:T(1,128)S(1)}, f32[1,2560]{1,0:T(1,128)}, u32[]{:S(2)}) copy-start(f32[1,2560]{1,0:T(1,128)} %get-tuple-element.136) | copy-start | bytes 30724
  731.0 101.1 %collective-permute-start.22 = (bf16[512,2560]{1,0:T(8,128)(2,1)}, bf16[512,2560]{1,0:T(8,128)(2,1)}, u32[]{:S(2)}, u32[]{:S(2)}) collective-permute-start(bf16[512,2560]{1,0:T(8,128)(2,1)} %get-tuple-element.130), channel_id=1, source_target_pairs={{0,2},{2,0},{1,3},{3,1},{4,6},{6,4},{5,7},{7,5}} | collective-permute-start | bytes 7864328 | tf_op jit(solution)/shard_map/ppermute | solution.py:872
  795.5 53.0 %collective-permute-start.17 = (bf16[1280,2048]{1,0:T(8,128)(2,1)}, bf16[1280,2048]{1,0:T(8,128)(2,1)}, u32[]{:S(2)}, u32[]{:S(2)}) collective-permute-start(bf16[1280,2048]{1,0:T(8,128)(2,1)} %get-tuple-element.125), channel_id=1, source_target_pairs={{0,1},{1,0},{2,3},{3,2},{4,5},{5,4},{6,7},{7,6}} | collective-permute-start | bytes 15728648 | tf_op jit(solution)/shard_map/ppermute | solution.py:872
  796.2 35.7 %collective-permute-start.26 = (f32[1,3072]{1,0:T(1,128)S(1)}, f32[1,3072]{1,0:T(1,128)S(1)}, u32[]{:S(2)}, u32[]{:S(2)}) collective-permute-start(f32[1,3072]{1,0:T(1,128)S(1)} %pad_maximum_fusion.1), channel_id=1, source_target_pairs={{0,1},{1,0},{2,3},{3,2},{4,5},{5,4},{6,7},{7,6}} | collective-permute-start | bytes 36872 | tf_op jit(solution)/shard_map/ppermute | solution.py:872
  796.7 35.8 %collective-permute-start.25 = (f32[1,2560]{1,0:T(1,128)S(1)}, f32[1,2560]{1,0:T(1,128)S(1)}, u32[]{:S(2)}, u32[]{:S(2)}) collective-permute-start(f32[1,2560]{1,0:T(1,128)S(1)} %copy-done.4), channel_id=1, source_target_pairs={{0,1},{1,0},{2,3},{3,2},{4,5},{5,4},{6,7},{7,6}} | collective-permute-start | bytes 30728 | tf_op jit(solution)/shard_map/ppermute | solution.py:872
  830.6 3.8 collective-permute-start.15
  832.0 5.6 collective-permute-start.23
  832.1 8.8 %collective-permute-start.24 = (bf16[512,2560]{1,0:T(8,128)(2,1)}, bf16[512,2560]{1,0:T(8,128)(2,1)}, u32[]{:S(2)}, u32[]{:S(2)}) collective-permute-start(bf16[512,2560]{1,0:T(8,128)(2,1)} %collective-permute-done.22.go_x), channel_id=1, source_target_pairs={{0,1},{1,0},{2,3},{3,2},{4,5},{5,4},{6,7},{7,6}} | collective-permute-start | bytes 7864328 | tf_op jit(solution)/shard_map/ppermute | solution.py:872
  832.5 12.2 %collective-permute-start.18 = (bf16[1280,1024]{1,0:T(8,128)(2,1)}, bf16[1280,1024]{1,0:T(8,128)(2,1)}, u32[]{:S(2)}, u32[]{:S(2)}) collective-permute-start(bf16[1280,1024]{1,0:T(8,128)(2,1)} %get-tuple-element.126), channel_id=1, source_target_pairs={{0,1},{1,0},{2,3},{3,2},{4,5},{5,4},{6,7},{7,6}} | collective-permute-start | bytes 7864328 | tf_op jit(solution)/shard_map/ppermute | solution.py:872
  834.4 14.0 %collective-permute-start.19 = (bf16[1280,1024]{1,0:T(8,128)(2,1)}, bf16[1280,1024]{1,0:T(8,128)(2,1)}, u32[]{:S(2)}, u32[]{:S(2)}) collective-permute-start(bf16[1280,1024]{1,0:T(8,128)(2,1)} %get-tuple-element.127), channel_id=1, source_target_pairs={{0,1},{1,0},{2,3},{3,2},{4,5},{5,4},{6,7},{7,6}} | collective-permute-start | bytes 7864328 | tf_op jit(solution)/shard_map/ppermute | solution.py:872
  837.5 38.6 %collective-permute-start.16 = (f32[1,1152]{1,0:T(1,128)S(1)}, f32[1,1152]{1,0:T(1,128)S(1)}, u32[]{:S(2)}, u32[]{:S(2)}) collective-permute-start(f32[1,1152]{1,0:T(1,128)S(1)} %add.94), channel_id=1, source_target_pairs={{0,1},{1,0},{2,3},{3,2},{4,5},{5,4},{6,7},{7,6}} | collective-permute-start | bytes 13832 | tf_op jit(solution)/shard_map/ppermute | solution.py:872
where the time goes:
time: 885 us; the launch traced here: 877 us
  Pallas kernels  674 us (76%)
  waiting for transfers between devices  134 us (15%)
  other arithmetic  20.8 us (2%)
  matrix products  20.4 us (2%)
  starting transfers between devices  14.5 us (2%)
  local copies, waits for them, and re-layouts  11.5 us (1%)
    pallas_call x2, Pallas kernels, bwd_call(): pl.pallas_call(bwd_kernel, grid_spec=pltpu.PrefetchScalarGridSpec(num_sca...  181 us
    ppermute x27, waiting for transfers between devices, swap(): return lax.ppermute(a, 'cp', perm)  134 us
    pallas_call x2, Pallas kernels, fwd_call(): pl.pallas_call(fwd_kernel, grid_spec=pltpu.PrefetchScalarGridSpec(num_sca...  97.3 us
    pallas_call x1, Pallas kernels, dhid_call(): pl.pallas_call(dhid_kernel, grid_spec=pltpu.PrefetchScalarGridSpec(num_sc...  76.6 us
    pallas_call x2, Pallas kernels, out_call(): pl.pallas_call(out_kernel, grid_spec=pltpu.PrefetchScalarGridSpec(num_sca...  68.9 us
    pallas_call x2, Pallas kernels, qkv_call(): pl.pallas_call(qkv_kernel, grid_spec=pltpu.PrefetchScalarGridSpec(num_sca...  65.6 us
    pallas_call x1, Pallas kernels, gqkv_call(): pl.pallas_call(gqkv_kernel, grid_spec=pltpu.PrefetchScalarGridSpec(num_sc...  63.8 us
    pallas_call x1, Pallas kernels, tail_call(): pl.pallas_call(tail_kernel, grid_spec=pltpu.PrefetchScalarGridSpec(num_sc...  27.6 us
  transfers between devices with their start and end apart: 27, of which 10 were waited for; matrix products, arithmetic and copies ran while one was open for 5% of the time, Pallas kernels for 72%

commit v1 on v0

--- a/solution.py
+++ b/solution.py
@@ -29,7 +29,8 @@
 LOG2E = 1.4426950408889634
 BF = jnp.bfloat16
 F32 = jnp.float32
-FAR = 1 << 20
+MIB = 1 << 20
+FAR = MIB
 SLOT = (0, 2, 1, 3)
 VMEM_MAX = 67043328
 
@@ -37,6 +38,10 @@
 SPERM = [(0, 1), (1, 0), (2, 3), (3, 2)]
 
 
+def pid():
+    return pl.program_id(0)
+
+
 def dot(a, b):
     return lax.dot_general(a, b, (((1,), (0,)), ((), ())), preferred_element_type=F32)
 
@@ -50,7 +55,7 @@
 
 
 def params(n_grid, **kw):
-    return pltpu.CompilerParams(dimension_semantics=("arbitrary",) * n_grid, vmem_limit_bytes=kw.pop("vmem", VMEM_MAX - (1 << 20)), **kw)
+    return pltpu.CompilerParams(dimension_semantics=("arbitrary",) * n_grid, vmem_limit_bytes=kw.pop("vmem", VMEM_MAX - MIB), **kw)
 
 
 def cost(flops, nbytes):
@@ -88,14 +93,14 @@
         in_specs=[pl.BlockSpec((1, ROWS, dv), lambda i: (i // POOL, i % POOL, 0)), const_spec((1, dv))],
         out_specs=[pl.BlockSpec((GRID, dv), lambda i: (i, 0))] * 2,
         out_shape=[jax.ShapeDtypeStruct((n * BLK, dv), BF)] * 2,
-        compiler_params=params(1),
+        compiler_params=params(1, vmem=12 * MIB),
         cost_estimate=cost(2 * HD2 * ROWS * dv, vis.size * 2),
         name="pool",
     )(vis, gain)
 
 
 def merge_kernel(tab, sc, soft, text, gain, x_ref, h_ref):
-    b = sc[0] * POOL + pl.program_id(0)
+    b = sc[0] * POOL + pid()
     ia, da, ib, db = tab[POOL * b], tab[POOL * b + 1], tab[POOL * b + 2], tab[POOL * b + 3]
     some = (da < FAR) | (db < FAR)
 
@@ -134,7 +139,7 @@
             out_specs=[spec, spec],
         ),
         out_shape=[jax.ShapeDtypeStruct((rows, d), BF)] * 2,
-        compiler_params=params(1),
+        compiler_params=params(1, vmem=26 * MIB),
         cost_estimate=cost(2 * rows * HD2 * d, (rows * 3 + soft.shape[0]) * d * 2),
         name="merge",
     )(tab, rr, soft, text, gain)
@@ -150,7 +155,7 @@
 def qkv_kernel(sc, ha, hb, wq, wk, wv, qg, kg, cos_ref, sin_ref, *rest):
     outs = rest[-NBUF:]
     q_o, qr_o, k_o, kr_o, v_o = outs[0:2], outs[2:POOL], outs[POOL:6], outs[6:8], outs[8:NBUF]
-    hid = jnp.where(pl.program_id(0) < 2, ha[ALL], hb[ALL])
+    hid = jnp.where(pid() < 2, ha[ALL], hb[ALL])
     cos, sin = cos_ref[ALL], sin_ref[ALL]
     for g in range(2):
         aq = dot(hid, wq[:, HD2 * g : HD2 * g + HD2]).astype(BF)
@@ -201,7 +206,7 @@
         ),
         out_shape=[jax.ShapeDtypeStruct((seq, w), BF) for w in widths],
         input_output_aliases=alias,
-        compiler_params=params(1),
+        compiler_params=params(1, vmem=40 * MIB),
         cost_estimate=cost(2 * CHIP * d * CHIP, CHIP * (d + 3584) * 2 + d * CHIP * 2),
         name="qkv",
     )(*args)
@@ -212,7 +217,7 @@
 
 
 def fwd_kernel(nkv, q_ref, k_ref, v_ref, bs_ref, o_ref, lse_ref, m_s, l_s, acc_s):
-    i = pl.program_id(0)
+    i = pid()
     m_s[ALL] = jnp.full(m_s.shape, NEG_BIG, F32)
     l_s[ALL] = jnp.zeros(l_s.shape, F32)
     acc_s[ALL] = jnp.zeros(acc_s.shape, F32)
@@ -276,7 +281,7 @@
             scratch_shapes=[pltpu.VMEM((2, QB, LANES), F32), pltpu.VMEM((2, QB, LANES), F32), pltpu.VMEM((2, QB, HD), F32)],
         ),
         out_shape=[jax.ShapeDtypeStruct((seq, HD2), BF), jax.ShapeDtypeStruct((n, 2, QB), F32)],
-        compiler_params=params(1),
+        compiler_params=params(1, vmem=18 * MIB),
         cost_estimate=cost(2 * 2 * 2 * seq * seq * HD * 0.7, seq * 1536 * 2),
         name="attn_fwd",
     )(nkv, q, k, v, bs_col)
@@ -301,7 +306,7 @@
     dy = dy_ref[ALL].astype(F32)
     dyn = dy * n
 
-    @pl.when(pl.program_id(0) == 0)
+    @pl.when(pid() == 0)
     def _():
         gp_ref[ALL] = jnp.zeros_like(gp_ref)
 
@@ -338,7 +343,7 @@
         out_shape=[jax.ShapeDtypeStruct((rows, d), BF)] * (1 + extra)
         + [jax.ShapeDtypeStruct((rows, HD2), BF)] * POOL
         + [jax.ShapeDtypeStruct((1, d), F32)],
-        compiler_params=params(1),
+        compiler_params=params(1, vmem=40 * MIB),
         cost_estimate=cost(POOL * rows * d * CHIP, rows * d * 2 * 5 + wo.size * 2),
         name="out_proj",
     )(sc, oo[0], oo[1], osib[0], osib[1], wo, dy, gain, *x)
@@ -359,7 +364,7 @@
     sc, q_ref, do_a, do_b, do_c, do_d, o_ref, k_ref, v_ref, lse_ref, bs_ref, qr_ref, kr_ref, cos_ref, sin_ref, qg, kg,
     out_ref, gq_ref, gk_ref, do_s, dl_s, dq_s, dk_s, dv_s, sem,
 ):
-    j = pl.program_id(0)
+    j = pid()
     nj = pl.num_programs(0)
 
     @pl.when(j == 0)
@@ -487,14 +492,14 @@
             jax.ShapeDtypeStruct((1, HD), F32),
             jax.ShapeDtypeStruct((1, HD), F32),
         ],
-        compiler_params=params(1),
+        compiler_params=params(1, vmem=53 * MIB),
         cost_estimate=cost(5 * 2 * 2 * seq * seq * HD * 0.6, seq * 4000 * 2),
         name="attn_bwd",
     )(sc, q, *dos, o, k, v, lse, bs_row, qr, kr, cos, sin, qg, kg)
 
 
 def gwo_kernel(sc, o0, o1, dp0, dp1, dp2, dp3, out_ref, full_ref, acc):
-    s = pl.program_id(0)
+    s = pid()
     o = jnp.where(sc[0] == 0, o0[ALL], o1[ALL])
 
     @pl.when(s == 0)
@@ -528,7 +533,7 @@
             scratch_shapes=[pltpu.VMEM((HD2, d), F32)],
         ),
         out_shape=[jax.ShapeDtypeStruct((HD2, d), BF), jax.ShapeDtypeStruct((CHIP, d), BF)],
-        compiler_params=params(1),
+        compiler_params=params(1, vmem=32 * MIB),
         cost_estimate=cost(2 * seq * HD2 * d, seq * (d + ROWS) * 2),
         name="grad_wo",
     )(sc, o0, o1, *dps)
@@ -591,14 +596,14 @@
             scratch_shapes=[pltpu.VMEM((mrow, SEQ), F32)],
         ),
         out_shape=[jax.ShapeDtypeStruct((half, w), BF) for w in outs] + [jax.ShapeDtypeStruct((2 * half, w), BF) for w in outs],
-        compiler_params=params(2),
+        compiler_params=params(2, vmem=54 * MIB),
         cost_estimate=cost(2 * seq * half * SEQ, seq * SEQ * POOL + half * SEQ * 2),
         name="grad_wqkv",
     )(sc, *hids, *parts)
 
 
 def dhid_kernel(sc, p0, p1, s0, s1, wq, wk, wv, xa, xb, dya, dyb, bs, gain, dm_ref, dx_ref, gp_ref, dq_s, dk_s, dv_s, dh_s):
-    i = pl.program_id(0)
+    i = pid()
     nb = pl.num_programs(0) // 2
     own_chip = (i // nb) == sc[0]
     c = sc[1]
@@ -679,14 +684,14 @@
             jax.ShapeDtypeStruct((rows, d), BF),
             jax.ShapeDtypeStruct((1, d), F32),
         ],
-        compiler_params=params(1),
+        compiler_params=params(1, vmem=54 * MIB),
         cost_estimate=cost(2 * 2 * rows * d * SEQ, rows * 2 * d * 8 + d * SEQ * 2),
         name="d_hidden",
     )(sc, *parts, wq, wk, wv, x_mine, x_peer, dy_mine, dy_peer, bs_col, gain)
 
 
 def dsoft_kernel(sc, own_ref, sib_ref, out_ref, buf, sem):
-    n = pl.program_id(0)
+    n = pid()
     c = sc[0]
     last = pl.num_programs(0) - 1
 
@@ -737,14 +742,14 @@
             scratch_shapes=[pltpu.VMEM((2, HD2, d), BF), pltpu.SemaphoreType.DMA((2, 2))],
         ),
         out_shape=jax.ShapeDtypeStruct((CHIP, d), BF),
-        compiler_params=params(1),
+        compiler_params=params(1, vmem=24 * MIB),
         cost_estimate=cost(2 * CHIP * HD2 * d, 3 * CHIP * d * 2),
         name="d_soft",
     )(sc, dm_own, dm_sib)
 
 
 def dvis_kernel(sc, ds_ref, wp, pooled_ref, gain, out_ref, gp_ref, dp_s):
-    i = pl.program_id(0)
+    i = pid()
 
     @pl.when(i == 0)
     def _():
@@ -783,14 +788,14 @@
             scratch_shapes=[pltpu.VMEM((n, dv), BF)],
         ),
         out_shape=[jax.ShapeDtypeStruct((n // BLK, GRID * GRID, dv), BF), jax.ShapeDtypeStruct((1, dv), F32)],
-        compiler_params=params(1),
+        compiler_params=params(1, vmem=24 * MIB),
         cost_estimate=cost(2 * n * d * dv + 2 * n * SIDE * HD * dv, n * SIDE * dv * 2 + wp.size * 2),
         name="d_vis",
     )(sc, d_soft, wp, pooled, gain)
 
 
 def tail_kernel(sc, normed, ds, sq, sk, sv, go_x, go_s, go_d, fq_in, fk_in, fv_in, fo_in, out_ref, fq, fk, fv, fo, sem):
-    i = pl.program_id(0)
+    i = pid()
     row = pl.multiple_of(sc[0] + i * HD, HD)
     orow = jnp.minimum(i, 3) * LANES
     cps = [pltpu.make_async_copy(src, dst.at[pl.ds(row, HD), :], sem.at[n]) for n, (src, dst) in enumerate(((sq, fq), (sk, fk), (sv, fv)))]
@@ -823,7 +828,7 @@
         ),
         out_shape=[jax.ShapeDtypeStruct((dv, d), BF)] + [jax.ShapeDtypeStruct(f.shape, BF) for f in fulls],
         input_output_aliases={9 + n: 1 + n for n in range(POOL)},
-        compiler_params=params(1),
+        compiler_params=params(1, vmem=32 * MIB),
         cost_estimate=cost(2 * tok * dv * d, tok * (d + dv) * 2 + dv * d * 2),
         name="tail",
     )(sc, normed, ds, *halves, *quarters, *fulls)

time: 885 us -> 882 us (level)
  Pallas kernels: 674 us -> 639 us
  local copies, waits for them, and re-layouts: 11.5 us -> 46 us
    unnamed x36 -> x94, local copies, waits for them, and re-layouts: 1.03 us -> 39.6 us
  transfers between devices with their start and end apart: 27 -> 27, of which waited for: 10 -> 11; matrix products, arithmetic and copies ran while one was open for 5% -> 4% of each run, Pallas kernels for 72% -> 69%
where the time goes in v1:
time: 882 us; the launch traced here: 873 us
  Pallas kernels  639 us (72%)
  waiting for transfers between devices  140 us (16%)
  local copies, waits for them, and re-layouts  46 us (5%)
  matrix products  17.9 us (2%)
  other arithmetic  14.6 us (2%)
  starting transfers between devices  14.4 us (2%)
    pallas_call x2, Pallas kernels, bwd_call(): pl.pallas_call(bwd_kernel, grid_spec=pltpu.PrefetchScalarGridSpec(num_sca...  181 us
    ppermute x27, waiting for transfers between devices, swap(): return lax.ppermute(a, 'cp', perm)  140 us
    pallas_call x2, Pallas kernels, fwd_call(): pl.pallas_call(fwd_kernel, grid_spec=pltpu.PrefetchScalarGridSpec(num_sca...  90.5 us
    pallas_call x1, Pallas kernels, dhid_call(): pl.pallas_call(dhid_kernel, grid_spec=pltpu.PrefetchScalarGridSpec(num_sc...  76.6 us
    pallas_call x2, Pallas kernels, out_call(): pl.pallas_call(out_kernel, grid_spec=pltpu.PrefetchScalarGridSpec(num_sca...  67.4 us
    pallas_call x1, Pallas kernels, gqkv_call(): pl.pallas_call(gqkv_kernel, grid_spec=pltpu.PrefetchScalarGridSpec(num_sc...  63.8 us
    pallas_call x2, Pallas kernels, qkv_call(): pl.pallas_call(qkv_kernel, grid_spec=pltpu.PrefetchScalarGridSpec(num_sca...  63.6 us
    unnamed x94, local copies, waits for them, and re-layouts  39.6 us
  transfers between devices with their start and end apart: 27, of which 11 were waited for; matrix products, arithmetic and copies ran while one was open for 4% of the time, Pallas kernels for 69%

profile of v1, /device:TPU:0, one launch (start us, length us, event | category | flops | bytes accessed | tf_op | source)
XLA Modules:
  0.0 873.3 jit_solution(6303921106763935295)
XLA Ops:
  0.6 0.7 reshape.136.gain_ref.gain
  1.3 6.4 copy-done.3
  7.7 5.3 pool.1
  13.0 1.0 copy-done.15
  14.0 3.3 collective-permute-start
  17.3 26.0 %collective-permute-done = bf16[512,1152]{1,0:T(8,128)(2,1)S(1)} collective-permute-done((bf16[512,1152]{1,0:T(8,128)(2,1)S(1)}, bf16[512,1152]{1,0:T(8,128)(2,1)S(1)}, u32[]{:S(2)}, u32[]{:S(2)}) %collective-permute-start) | collective-permute-done | bytes 1179680 | tf_op jit(solution)/shard_map/ppermute | solution.py:877
  43.3 1.6 pad_maximum_fusion
  44.9 1.7 collective-permute-start.2
  46.7 0.6 and_select_fusion.1
  48.4 1.4 collective-permute-done.1
  49.8 1.4 slice_dynamic-update-slice_fusion.1
  51.2 1.4 slice_dynamic-update-slice_fusion
  52.7 17.9 %convolution_convert_fusion.soft = bf16[2048,2560]{1,0:T(8,128)(2,1)S(1)} fusion(bf16[2048,1152]{1,0:T(8,128)(2,1)S(1)} %bitcast.37, bf16[1152,2560]{1,0:T(8,128)(2,1)} %wp.1), kind=kOutput, calls=%fused_computation | convolution fusion | flops 12084838400 | bytes 21102592 | tf_op jit(solution)/shard_map/dot_general | solution.py:888
  70.7 8.1 merge.3
  78.7 2.4 copy-done.9
  81.1 1.6 collective-permute-start.4
  82.7 78.0 %collective-permute-done.2.text = bf16[1024,2560]{1,0:T(8,128)(2,1)} collective-permute-done((bf16[1024,2560]{1,0:T(8,128)(2,1)}, bf16[1024,2560]{1,0:T(8,128)(2,1)}, u32[]{:S(2)}, u32[]{:S(2)}) %collective-permute-start.2) | collective-permute-done | bytes 5242912 | tf_op jit(solution)/shard_map/ppermute | solution.py:877
  160.7 9.7 %merge.2 = (bf16[1024,2560]{1,0:T(8,128)(2,1)S(1)}, bf16[1024,2560]{1,0:T(8,128)(2,1)}) custom-call(s32[64]{0:T(128)S(1)} %reshape.134.tab, s32[1]{0:T(128)} %bitcast.9.sc, bf16[2048,2560]{1,0:T(8,128)(2,1)S(1)} %convolution_convert_fusion.soft, bf16[1024,2560]{1,0:T(8,128)(2,1)} %collective-permute-done.2.text, f32[1,2560]{1,0:T(1,128)S(1)} %reshape.137.gain), custom_call_target="tpu_custom_call" | custom-call | flops 2684354560 | bytes 26214400 | tf_op jit(solution)/shard_map/merge/pallas_call | solution.py:133
  170.4 2.3 copy-done.10
  172.8 1.4 collective-permute-start.7
  174.4 0.6 copy.47.bs_ref.bs
  175.5 9.3 %multiply_sine_fusion = (f32[4096,128]{1,0:T(8,128)}, f32[4096,128]{1,0:T(8,128)}) fusion(f32[128]{0:T(128)S(1)} %multiply_power_fusion, f32[4096]{0:T(1024)S(1)} %convert_multiply_fusion), kind=kLoop, calls=%fused_computation.1 | loop fusion | flops 524288 | bytes 4211200 | tf_op jit(solution)/shard_map/sin | solution.py:896
  184.8 31.8 %qkv.2 = (bf16[4096,512]{1,0:T(8,128)(2,1)}, bf16[4096,512]{1,0:T(8,128)(2,1)}, bf16[4096,512]{1,0:T(8,128)(2,1)}, bf16[4096,512]{1,0:T(8,128)(2,1)}, bf16[4096,...) custom-call(s32[2]{0:T(128)S(1)} %pad_add_fusion.1.sc, ...), custom_call_target="tpu_custom_call" | custom-call | flops 21474836480 | bytes 35651584 | tf_op jit(solution)/shard_map/qkv/pallas_call | solution.py:202
  216.5 31.8 %qkv.3 = (bf16[4096,512]{1,0:T(8,128)(2,1)}, bf16[4096,512]{1,0:T(8,128)(2,1)}, bf16[4096,512]{1,0:T(8,128)(2,1)}, bf16[4096,512]{1,0:T(8,128)(2,1)}, bf16[4096,...) custom-call(s32[2]{0:T(128)S(1)} %pad_add_fusion.2.sc, ...), custom_call_target="tpu_custom_call", output_to_operand_aliasing={{0}: (10, {}), {1}: (11, {}), {2}: (12, {}), {3}: (13, {}),... | custom-call | flops 21474836480 | bytes 35651584 | tf_op jit(solution)/shard_map/qkv/pallas_call | solution.py:202
  248.4 5.2 copy-done.19
  253.6 45.3 %attn_fwd.3 = (bf16[4096,512]{1,0:T(8,128)(2,1)S(1)}, f32[8,2,512]{2,1,0:T(2,128)S(1)}) custom-call(s32[8]{0:T(128)S(1)} %add_add_fusion.nkv, bf16[4096,512]{1,0:T(8,128)(2,1)S(1)} %copy-done.19, bf16[4096,256]{1,0:T(8,128)(2,1)S(1)} %get-tuple-element.98.k_ref, bf16[4096,256]{1,0:T(8,128)(2,1)S(1)} %get-tuple-element.99.v_ref, s32[4096,1]{1,0:T(8,128)S(1)} %copy.47.bs_ref.bs), custom_call_target="tpu_custom_call" | custom-call | flops 24051816448 | bytes 12582912 | tf_op jit(solution)/shard_map/attn_fwd/pallas_call | solution.py:269
  299.1 45.1 %attn_fwd.2 = (bf16[4096,512]{1,0:T(8,128)(2,1)S(1)}, f32[8,2,512]{2,1,0:T(2,128)S(1)}) custom-call(s32[8]{0:T(128)S(1)} %add_add_fusion.nkv, bf16[4096,512]{1,0:T(8,128)(2,1)S(1)} %copy-done.18, bf16[4096,256]{1,0:T(8,128)(2,1)S(1)} %get-tuple-element.94.k_ref, bf16[4096,256]{1,0:T(8,128)(2,1)S(1)} %get-tuple-element.95.v_ref, s32[4096,1]{1,0:T(8,128)S(1)} %copy.47.bs_ref.bs), custom_call_target="tpu_custom_call" | custom-call | flops 24051816448 | bytes 12582912 | tf_op jit(solution)/shard_map/attn_fwd/pallas_call | solution.py:269
  344.8 6.7 collective-permute-done.5.os0
  351.5 2.0 copy-done.38
  353.5 33.2 %out_proj.3 = (bf16[1024,2560]{1,0:T(8,128)(2,1)}, bf16[1024,512]{1,0:T(8,128)(2,1)S(1)}, bf16[1024,512]{1,0:T(8,128)(2,1)S(1)}, bf16[1024,512]{1,0:T(8,128)(2,1...) custom-call(s32[2]{0:T(128)S(1)} %pad_add_fusion.2.sc, ...), custom_call_target="tpu_custom_call" | custom-call | flops 21474836480 | bytes 36700160 | tf_op jit(solution)/shard_map/out_proj/pallas_call | solution.py:335
  386.8 1.0 copy-done.28
  387.7 1.0 copy-done.29
  389.1 34.2 %out_proj.2 = (bf16[1024,2560]{1,0:T(8,128)(2,1)}, bf16[1024,2560]{1,0:T(8,128)(2,1)}, bf16[1024,512]{1,0:T(8,128)(2,1)S(1)}, bf16[1024,512]{1,0:T(8,128)(2,1)S(...) custom-call(s32[2]{0:T(128)S(1)} %pad_add_fusion.1.sc, ...), custom_call_target="tpu_custom_call" | custom-call | flops 21474836480 | bytes 36700160 | tf_op jit(solution)/shard_map/out_proj/pallas_call | solution.py:335
  423.3 1.0 copy-done.26
  424.2 1.0 copy-done.27
  426.0 1.8 collective-permute-done.10.do_c
  427.9 1.0 copy-done.42
  428.9 90.8 %attn_bwd.3 = (bf16[4096,1024]{1,0:T(8,128)(2,1)}, f32[1,256]{1,0:T(1,128)S(1)}, f32[1,256]{1,0:T(1,128)S(1)}) custom-call(s32[9]{0:T(128)S(1)} %pad_add_fusion.3.sc, bf16[4096,512]{1,0:T(8,128)(2,1)} %get-tuple-element.97.q_ref, bf16[1024,512]{1,0:T(8,128)(2,1)} %copy-done.27, bf16[1024,512]{1,0:T(8,128)(2,1)} %copy-done.29, bf16[1024,512]{1,0:T(8,128)(2,1)} %copy-done.42, ...), custom_call_target="tpu_custom_call" | custom-call | flops 51539607552 | bytes 32768000 | tf_op jit(solution)/shard_map/attn_bwd/pallas_call | solution.py:453
  519.8 0.9 copy-done.39
  521.1 90.4 %attn_bwd.2 = (bf16[4096,1024]{1,0:T(8,128)(2,1)}, f32[1,256]{1,0:T(1,128)S(1)}, f32[1,256]{1,0:T(1,128)S(1)}) custom-call(s32[9]{0:T(128)S(1)} %pad_add_fusion.3.sc, bf16[4096,512]{1,0:T(8,128)(2,1)} %get-tuple-element.93.q_ref, bf16[1024,512]{1,0:T(8,128)(2,1)} %copy-done.26, bf16[1024,512]{1,0:T(8,128)(2,1)} %copy-done.28, bf16[1024,512]{1,0:T(8,128)(2,1)} %copy-done.40, ...), custom_call_target="tpu_custom_call" | custom-call | flops 51539607552 | bytes 32768000 | tf_op jit(solution)/shard_map/attn_bwd/pallas_call | solution.py:453
  612.5 12.5 %collective-permute-done.12.s0 = bf16[4096,1024]{1,0:T(8,128)(2,1)S(1)} collective-permute-done((bf16[4096,1024]{1,0:T(8,128)(2,1)}, bf16[4096,1024]{1,0:T(8,128)(2,1)S(1)}, u32[]{:S(2)}, u32[]{:S(2)}) %collective-permute-start.12) | collective-permute-done | bytes 8388640 | tf_op jit(solution)/shard_map/ppermute | solution.py:877
  625.0 3.3 copy-done.36
  628.3 76.6 %d_hidden.1 = (bf16[2048,2560]{1,0:T(8,128)(2,1)}, bf16[1024,2560]{1,0:T(8,128)(2,1)}, f32[1,2560]{1,0:T(1,128)}) custom-call(s32[2]{0:T(128)} %copy-done.17, bf16[4096,1024]{1,0:T(8,128)(2,1)} %get-tuple-element.110.p0, bf16[4096,1024]{1,0:T(8,128)(2,1)} %get-tuple-element.118.p1, bf16[4096,1024]{1,0:T(8,128)(2,1)} %copy-done.36, ...), custom_call_target="tpu_custom_call" | custom-call | flops 42949672960 | bytes 62914560 | tf_op jit(solution)/shard_map/d_hidden/pallas_call | solution.py:661
  705.4 0.6 pad_add_fusion.6.sc
  706.1 2.2 copy-done.12
  708.2 2.2 copy-done.14
  710.4 22.1 %grad_wo.1 = (bf16[512,2560]{1,0:T(8,128)(2,1)}, bf16[2048,2560]{1,0:T(8,128)(2,1)}) custom-call(s32[7]{0:T(128)S(1)} %stack.104.sc, bf16[4096,512]{1,0:T(8,128)(2,1)S(1)} %copy-done.14, bf16[4096,512]{1,0:T(8,128)(2,1)S(1)} %copy-done.12, bf16[1024,2560]{1,0:T(8,128)(2,1)} %get-tuple-element.128.dp0, bf16[1024,2560]{1,0:T(8,128)(2,1)} %get-tuple-element.129.dp1, ...), custom_call_target="tpu_custom_call" | custom-call | flops 10737418240 | bytes 29360128 | tf_op jit(solution)/shard_map/grad_wo/pallas_call | solution.py:526
  732.5 0.7 collective-permute-start.22
  733.2 63.8 %grad_wqkv.1 = (bf16[1280,2048]{1,0:T(8,128)(2,1)}, bf16[1280,1024]{1,0:T(8,128)(2,1)}, bf16[1280,1024]{1,0:T(8,128)(2,1)}, bf16[2560,2048]{1,0:T(8,128)(2,1)}, ...) custom-call(s32[3]{0:T(128)} %pad_add_fusion.6.sc, bf16[1024,2560]{1,0:T(8,128)(2,1)} %get-tuple-element.82.ha.h0, ...), custom_call_target="tpu_custom_call" | custom-call | flops 42949672960 | bytes 77594624 | tf_op jit(solution)/shard_map/grad_wqkv/pallas_call | solution.py:588
  797.8 4.0 copy-done.4
  801.8 11.8 %d_soft.1.ds_ref.ds = bf16[2048,2560]{1,0:T(8,128)(2,1)S(1)} custom-call(s32[17]{0:T(128)S(1)} %pad_add_fusion.4.sc, bf16[2048,2560]{1,0:T(8,128)(2,1)S(1)} %copy-done.4, bf16[2048,2560]{1,0:T(8,128)(2,1)} %collective-permute-done.14.sib_ref), custom_call_target="tpu_custom_call" | custom-call | flops 5368709120 | bytes 31457280 | tf_op jit(solution)/shard_map/d_soft/pallas_call | solution.py:735
  813.6 14.0 %d_vis.1 = (bf16[2,4096,1152]{2,1,0:T(8,128)(2,1)}, f32[1,1152]{1,0:T(1,128)S(1)}) custom-call(s32[1]{0:T(128)} %bitcast.15.sc, bf16[2048,2560]{1,0:T(8,128)(2,1)S(1)} %d_soft.1.ds_ref.ds, bf16[1152,2560]{1,0:T(8,128)(2,1)S(1)} %bitcast.44, bf16[512,1152]{1,0:T(8,128)(2,1)S(1)} %copy-done.16, f32[1,1152]{1,0:T(1,128)S(1)} %copy-done.8), custom_call_target="tpu_custom_call" | custom-call | flops 7851737088 | bytes 24772608 | tf_op jit(solution)/shard_map/d_vis/pallas_call | solution.py:776
  827.7 1.4 collective-permute-start.15
  829.6 1.7 collective-permute-done.15
  831.4 0.5 slice_reduce_fusion.1
  831.9 0.6 slice_reduce_fusion
  832.6 0.6 convert_reduce_fusion
  833.2 1.1 collective-permute-done.23.go_s
  834.4 3.6 collective-permute-done.24.go_d
  838.0 3.7 collective-permute-done.18.sk
  841.8 3.7 collective-permute-done.19.sv
  845.5 2.3 copy-done.2
  847.9 24.6 %tail.1 = (bf16[1152,2560]{1,0:T(8,128)(2,1)}, bf16[2560,2048]{1,0:T(8,128)(2,1)}, bf16[2560,1024]{1,0:T(8,128)(2,1)}, bf16[2560,1024]{1,0:T(8,128)(2,1)}, bf16[2048,2560]{1,0:T(8,128)(2,1)}) custom-call(s32[4]{0:T(128)S(1)} %pad_add_fusion.5.sc, ...), custom_call_target="tpu_custom_call", output_to_operand_aliasing={{1}: (9, {}), {2}: (10, {}), {3}: (11, {}), {4}: (12, {})} | custom-call | flops 12079595520 | bytes 21102592 | tf_op jit(solution)/shard_map/tail/pallas_call | solution.py:817
  872.5 0.6 convert_reduce_fusion.1
  (151 shorter events, 7.0 us)
Async XLA Ops:
  1.3 6.4 copy-start.3
  7.7 5.3 copy-start.7
  14.0 32.7 %copy-start.30 = (s32[8]{0:T(128)S(1)}, s32[8]{0:T(128)}, u32[]{:S(2)}) copy-start(s32[8]{0:T(128)} %param.16) | copy-start | bytes 100
  14.0 33.7 %copy-start.32 = (bf16[2560]{0:T(1024)(128)(2,1)S(1)}, bf16[2560]{0:T(1024)(128)(2,1)}, u32[]{:S(2)}) copy-start(bf16[2560]{0:T(1024)(128)(2,1)} %param.20) | copy-start | bytes 15364
  14.0 29.3 %collective-permute-start = (bf16[512,1152]{1,0:T(8,128)(2,1)S(1)}, bf16[512,1152]{1,0:T(8,128)(2,1)S(1)}, u32[]{:S(2)}, u32[]{:S(2)}) collective-permute-start(bf16[512,1152]{1,0:T(8,128)(2,1)S(1)} %get-tuple-element.80), channel_id=1, source_target_pairs={{0,2},{2,0},{1,3},{3,1},{4,6},{6,4},{5,7},{7,5}} | collective-permute-start | bytes 3538952 | tf_op jit(solution)/shard_map/ppermute | solution.py:877
  44.9 4.9 collective-permute-start.1
  44.9 115.8 %collective-permute-start.2 = (bf16[1024,2560]{1,0:T(8,128)(2,1)}, bf16[1024,2560]{1,0:T(8,128)(2,1)}, u32[]{:S(2)}, u32[]{:S(2)}) collective-permute-start(bf16[1024,2560]{1,0:T(8,128)(2,1)} %text.1), channel_id=1, source_target_pairs={{0,2},{2,0},{1,3},{3,1},{4,6},{6,4},{5,7},{7,5}} | collective-permute-start | bytes 15728648 | tf_op jit(solution)/shard_map/ppermute | solution.py:877
  47.7 113.0 %copy-start.6 = (f32[1,2560]{1,0:T(1,128)}, f32[1,2560]{1,0:T(1,128)S(1)}, u32[]{:S(2)}) copy-start(f32[1,2560]{1,0:T(1,128)S(1)} %reshape.137.gain) | copy-start | bytes 30724
  52.7 18.0 %copy-start.1 = (bf16[4,512,1152]{2,1,0:T(8,128)(2,1)}, bf16[4,512,1152]{2,1,0:T(8,128)(2,1)S(1)}, u32[]{:S(2)}) copy-start(bf16[4,512,1152]{2,1,0:T(8,128)(2,1)S(1)} %slice_dynamic-update-slice_fusion) | copy-start | bytes 14155780
  78.7 2.4 copy-start.9
  81.1 103.7 %collective-permute-start.4 = (bf16[1024,2560]{1,0:T(8,128)(2,1)}, bf16[1024,2560]{1,0:T(8,128)(2,1)}, u32[]{:S(2)}, u32[]{:S(2)}) collective-permute-start(bf16[1024,2560]{1,0:T(8,128)(2,1)} %get-tuple-element.82.ha.h0), channel_id=1, source_target_pairs={{0,1},{1,0},{2,3},{3,2},{4,5},{5,4},{6,7},{7,6}} | collective-permute-start | bytes 15728648 | tf_op jit(solution)/shard_map/ppermute | solution.py:877
  160.7 13.5 %copy-start.43 = (bf16[256]{0:T(256)(128)(2,1)S(1)}, bf16[256]{0:T(256)(128)(2,1)}, u32[]{:S(2)}) copy-start(bf16[256]{0:T(256)(128)(2,1)} %param.24) | copy-start | bytes 1540
  160.7 13.5 %copy-start.44 = (bf16[256]{0:T(256)(128)(2,1)S(1)}, bf16[256]{0:T(256)(128)(2,1)}, u32[]{:S(2)}) copy-start(bf16[256]{0:T(256)(128)(2,1)} %param.25) | copy-start | bytes 1540
  170.4 2.4 copy-start.10
  172.8 43.8 %collective-permute-start.3 = (bf16[1024,2560]{1,0:T(8,128)(2,1)}, bf16[1024,2560]{1,0:T(8,128)(2,1)}, u32[]{:S(2)}, u32[]{:S(2)}) collective-permute-start(bf16[1024,2560]{1,0:T(8,128)(2,1)} %get-tuple-element.81.ha.h2), channel_id=1, source_target_pairs={{0,1},{1,0},{2,3},{3,2},{4,5},{5,4},{6,7},{7,6}} | collective-permute-start | bytes 15728648 | tf_op jit(solution)/shard_map/ppermute | solution.py:877
  172.8 172.0 %collective-permute-start.7 = (bf16[1024,2560]{1,0:T(8,128)(2,1)}, bf16[1024,2560]{1,0:T(8,128)(2,1)}, u32[]{:S(2)}, u32[]{:S(2)}) collective-permute-start(bf16[1024,2560]{1,0:T(8,128)(2,1)} %dya.1), channel_id=1, source_target_pairs={{0,2},{2,0},{1,3},{3,1},{4,6},{6,4},{5,7},{7,5}} | collective-permute-start | bytes 15728648 | tf_op jit(solution)/shard_map/ppermute | solution.py:877
  175.1 124.0 %copy-start.5 = (s32[4096,1]{1,0:T(8,128)}, s32[4096,1]{1,0:T(8,128)S(1)}, u32[]{:S(2)}) copy-start(s32[4096,1]{1,0:T(8,128)S(1)} %copy.47.bs_ref.bs) | copy-start | bytes 49156
  175.2 213.9 %copy-start.17 = (s32[2]{0:T(128)}, s32[2]{0:T(128)S(1)}, u32[]{:S(2)}) copy-start(s32[2]{0:T(128)S(1)} %pad_add_fusion.1.sc) | copy-start | bytes 28
  248.3 50.6 %copy-start.21 = (bf16[4096,256]{1,0:T(8,128)(2,1)}, bf16[4096,256]{1,0:T(8,128)(2,1)S(1)}, u32[]{:S(2)}) copy-start(bf16[4096,256]{1,0:T(8,128)(2,1)S(1)} %get-tuple-element.98.k_ref) | copy-start | bytes 6291460
  248.3 50.6 %copy-start.22 = (bf16[4096,256]{1,0:T(8,128)(2,1)}, bf16[4096,256]{1,0:T(8,128)(2,1)S(1)}, u32[]{:S(2)}) copy-start(bf16[4096,256]{1,0:T(8,128)(2,1)S(1)} %get-tuple-element.109.kr_ref) | copy-start | bytes 6291460
  248.4 50.6 %copy-start.23 = (bf16[4096,256]{1,0:T(8,128)(2,1)}, bf16[4096,256]{1,0:T(8,128)(2,1)S(1)}, u32[]{:S(2)}) copy-start(bf16[4096,256]{1,0:T(8,128)(2,1)S(1)} %get-tuple-element.117.kr_ref) | copy-start | bytes 6291460
  248.4 50.6 %copy-start.25 = (bf16[4096,256]{1,0:T(8,128)(2,1)}, bf16[4096,256]{1,0:T(8,128)(2,1)S(1)}, u32[]{:S(2)}) copy-start(bf16[4096,256]{1,0:T(8,128)(2,1)S(1)} %get-tuple-element.99.v_ref) | copy-start | bytes 6291460
  248.4 50.7 %copy-start.20 = (bf16[4096,256]{1,0:T(8,128)(2,1)}, bf16[4096,256]{1,0:T(8,128)(2,1)S(1)}, u32[]{:S(2)}) copy-start(bf16[4096,256]{1,0:T(8,128)(2,1)S(1)} %get-tuple-element.94.k_ref) | copy-start | bytes 6291460
  248.4 50.7 %copy-start.24 = (bf16[4096,256]{1,0:T(8,128)(2,1)}, bf16[4096,256]{1,0:T(8,128)(2,1)S(1)}, u32[]{:S(2)}) copy-start(bf16[4096,256]{1,0:T(8,128)(2,1)S(1)} %get-tuple-element.95.v_ref) | copy-start | bytes 6291460
  248.4 5.2 copy-start.19
  253.6 45.5 %copy-start.18 = (bf16[4096,512]{1,0:T(8,128)(2,1)S(1)}, bf16[4096,512]{1,0:T(8,128)(2,1)}, u32[]{:S(2)}) copy-start(bf16[4096,512]{1,0:T(8,128)(2,1)} %get-tuple-element.93.q_ref) | copy-start | bytes 12582916
  299.0 90.1 %copy-start.11 = (bf16[4096,512]{1,0:T(8,128)(2,1)}, bf16[4096,512]{1,0:T(8,128)(2,1)S(1)}, u32[]{:S(2)}) copy-start(bf16[4096,512]{1,0:T(8,128)(2,1)S(1)} %get-tuple-element.100.oo1.o_ref.o1) | copy-start | bytes 12582916
  299.0 45.8 %collective-permute-start.6 = (bf16[4096,512]{1,0:T(8,128)(2,1)S(1)}, bf16[4096,512]{1,0:T(8,128)(2,1)S(1)}, u32[]{:S(2)}, u32[]{:S(2)}) collective-permute-start(bf16[4096,512]{1,0:T(8,128)(2,1)S(1)} %get-tuple-element.100.oo1.o_ref.o1), channel_id=1, source_target_pairs={{0,1},{1,0},{2,3},{3,2},{4,5},{5,4},{6,7},{7,6}} | collective-permute-start | bytes 12582920 | tf_op jit(solution)/shard_map/ppermute | solution.py:877
  299.1 45.7 %copy-start.33 = (bf16[2560]{0:T(1024)(128)(2,1)S(1)}, bf16[2560]{0:T(1024)(128)(2,1)}, u32[]{:S(2)}) copy-start(bf16[2560]{0:T(1024)(128)(2,1)} %param.27) | copy-start | bytes 15364
  344.3 44.8 %copy-start.13 = (bf16[4096,512]{1,0:T(8,128)(2,1)}, bf16[4096,512]{1,0:T(8,128)(2,1)S(1)}, u32[]{:S(2)}) copy-start(bf16[4096,512]{1,0:T(8,128)(2,1)S(1)} %get-tuple-element.96.oo0.o_ref.o0) | copy-start | bytes 12582916
  344.3 7.3 collective-permute-start.5
  344.8 6.8 copy-start.37
  388.7 37.3 %collective-permute-start.11 = (bf16[1024,512]{1,0:T(8,128)(2,1)S(1)}, bf16[1024,512]{1,0:T(8,128)(2,1)S(1)}, u32[]{:S(2)}, u32[]{:S(2)}) collective-permute-start(bf16[1024,512]{1,0:T(8,128)(2,1)S(1)} %get-tuple-element.114), channel_id=1, source_target_pairs={{0,1},{1,0},{2,3},{3,2},{4,5},{5,4},{6,7},{7,6}} | collective-permute-start | bytes 3145736 | tf_op jit(solution)/shard_map/ppermute | solution.py:877
  425.2 2.7 collective-permute-start.10
  425.5 94.3 %collective-permute-start.9 = (bf16[1024,512]{1,0:T(8,128)(2,1)S(1)}, bf16[1024,512]{1,0:T(8,128)(2,1)S(1)}, u32[]{:S(2)}, u32[]{:S(2)}) collective-permute-start(bf16[1024,512]{1,0:T(8,128)(2,1)S(1)} %get-tuple-element.106), channel_id=1, source_target_pairs={{0,1},{1,0},{2,3},{3,2},{4,5},{5,4},{6,7},{7,6}} | collective-permute-start | bytes 3145736 | tf_op jit(solution)/shard_map/ppermute | solution.py:877
  425.9 93.9 %collective-permute-start.8 = (bf16[1024,512]{1,0:T(8,128)(2,1)S(1)}, bf16[1024,512]{1,0:T(8,128)(2,1)S(1)}, u32[]{:S(2)}, u32[]{:S(2)}) collective-permute-start(bf16[1024,512]{1,0:T(8,128)(2,1)S(1)} %get-tuple-element.105), channel_id=1, source_target_pairs={{0,1},{1,0},{2,3},{3,2},{4,5},{5,4},{6,7},{7,6}} | collective-permute-start | bytes 3145736 | tf_op jit(solution)/shard_map/ppermute | solution.py:877
  519.6 92.8 %collective-permute-start.13 = (bf16[4096,1024]{1,0:T(8,128)(2,1)}, bf16[4096,1024]{1,0:T(8,128)(2,1)}, u32[]{:S(2)}, u32[]{:S(2)}) collective-permute-start(bf16[4096,1024]{1,0:T(8,128)(2,1)} %get-tuple-element.118.p1), channel_id=1, source_target_pairs={{0,1},{1,0},{2,3},{3,2},{4,5},{5,4},{6,7},{7,6}} | collective-permute-start | bytes 25165832 | tf_op jit(solution)/shard_map/ppermute | solution.py:877
  611.6 13.4 %collective-permute-start.12 = (bf16[4096,1024]{1,0:T(8,128)(2,1)}, bf16[4096,1024]{1,0:T(8,128)(2,1)S(1)}, u32[]{:S(2)}, u32[]{:S(2)}) collective-permute-start(bf16[4096,1024]{1,0:T(8,128)(2,1)} %get-tuple-element.110.p0), channel_id=1, source_target_pairs={{0,1},{1,0},{2,3},{3,2},{4,5},{5,4},{6,7},{7,6}} | collective-permute-start | bytes 25165832 | tf_op jit(solution)/shard_map/ppermute | solution.py:877
  612.0 94.1 %collective-permute-start.21 = (bf16[1024,2560]{1,0:T(8,128)(2,1)}, bf16[1024,2560]{1,0:T(8,128)(2,1)}, u32[]{:S(2)}, u32[]{:S(2)}) collective-permute-start(bf16[1024,2560]{1,0:T(8,128)(2,1)} %get-tuple-element.129.dp1), channel_id=1, source_target_pairs={{0,1},{1,0},{2,3},{3,2},{4,5},{5,4},{6,7},{7,6}} | collective-permute-start | bytes 15728648 | tf_op jit(solution)/shard_map/ppermute | solution.py:877
  612.1 93.9 %collective-permute-start.20 = (bf16[1024,2560]{1,0:T(8,128)(2,1)}, bf16[1024,2560]{1,0:T(8,128)(2,1)}, u32[]{:S(2)}, u32[]{:S(2)}) collective-permute-start(bf16[1024,2560]{1,0:T(8,128)(2,1)} %get-tuple-element.128.dp0), channel_id=1, source_target_pairs={{0,1},{1,0},{2,3},{3,2},{4,5},{5,4},{6,7},{7,6}} | collective-permute-start | bytes 15728648 | tf_op jit(solution)/shard_map/ppermute | solution.py:877
  625.0 3.3 copy-start.36
  704.9 92.9 %collective-permute-start.14 = (bf16[2048,2560]{1,0:T(8,128)(2,1)}, bf16[2048,2560]{1,0:T(8,128)(2,1)}, u32[]{:S(2)}, u32[]{:S(2)}) collective-permute-start(bf16[2048,2560]{1,0:T(8,128)(2,1)} %get-tuple-element.121.own_ref), channel_id=1, source_target_pairs={{0,1},{1,0},{2,3},{3,2},{4,5},{5,4},{6,7},{7,6}} | collective-permute-start | bytes 31457288 | tf_op jit(solution)/shard_map/ppermute | solution.py:877
  706.0 2.2 copy-start.12
  708.2 2.2 copy-start.14
  710.4 103.2 %slice-start = ((s8[5898240]{0:T(1024)(128)(4,1)}), s8[4194304]{0:T(1024)(128)(4,1)S(1)}, s32[]{:S(2)}) async-start(s8[5898240]{0:T(1024)(128)(4,1)} %bitcast.43), calls=%async_computation | async-start | bytes 8388608
  732.5 64.6 %copy-start.34 = (s32[8]{0:T(128)S(1)}, s32[8]{0:T(128)}, u32[]{:S(2)}) copy-start(s32[8]{0:T(128)} %get-tuple-element.159) | copy-start | bytes 100
  732.5 64.6 %copy-start.35 = (s32[8]{0:T(128)S(1)}, s32[8]{0:T(128)}, u32[]{:S(2)}) copy-start(s32[8]{0:T(128)} %get-tuple-element.160) | copy-start | bytes 100
  732.5 65.2 %copy-start.31 = (f32[1,2560]{1,0:T(1,128)S(1)}, f32[1,2560]{1,0:T(1,128)}, u32[]{:S(2)}) copy-start(f32[1,2560]{1,0:T(1,128)} %get-tuple-element.136) | copy-start | bytes 30724
  732.5 81.1 %slice-start.1 = ((s8[5898240]{0:T(1024)(128)(4,1)}), s8[1703936]{0:T(1024)(128)(4,1)S(1)}, s32[]{:S(2)}) async-start(s8[5898240]{0:T(1024)(128)(4,1)} %bitcast.43), calls=%async_computation.1 | async-start | bytes 3407872
  732.5 96.5 %collective-permute-start.22 = (bf16[512,2560]{1,0:T(8,128)(2,1)}, bf16[512,2560]{1,0:T(8,128)(2,1)S(1)}, u32[]{:S(2)}, u32[]{:S(2)}) collective-permute-start(bf16[512,2560]{1,0:T(8,128)(2,1)} %get-tuple-element.130), channel_id=1, source_target_pairs={{0,2},{2,0},{1,3},{3,1},{4,6},{6,4},{5,7},{7,5}} | collective-permute-start | bytes 7864328 | tf_op jit(solution)/shard_map/ppermute | solution.py:877
  797.0 48.5 %collective-permute-start.17 = (bf16[1280,2048]{1,0:T(8,128)(2,1)}, bf16[1280,2048]{1,0:T(8,128)(2,1)}, u32[]{:S(2)}, u32[]{:S(2)}) collective-permute-start(bf16[1280,2048]{1,0:T(8,128)(2,1)} %get-tuple-element.125), channel_id=1, source_target_pairs={{0,1},{1,0},{2,3},{3,2},{4,5},{5,4},{6,7},{7,6}} | collective-permute-start | bytes 15728648 | tf_op jit(solution)/shard_map/ppermute | solution.py:877
  797.2 31.8 %collective-permute-start.26 = (f32[1,3072]{1,0:T(1,128)S(1)}, f32[1,3072]{1,0:T(1,128)S(1)}, u32[]{:S(2)}, u32[]{:S(2)}) collective-permute-start(f32[1,3072]{1,0:T(1,128)S(1)} %pad_maximum_fusion.1), channel_id=1, source_target_pairs={{0,1},{1,0},{2,3},{3,2},{4,5},{5,4},{6,7},{7,6}} | collective-permute-start | bytes 36872 | tf_op jit(solution)/shard_map/ppermute | solution.py:877
  797.7 31.8 %collective-permute-start.25 = (f32[1,2560]{1,0:T(1,128)S(1)}, f32[1,2560]{1,0:T(1,128)S(1)}, u32[]{:S(2)}, u32[]{:S(2)}) collective-permute-start(f32[1,2560]{1,0:T(1,128)S(1)} %copy-done.31), channel_id=1, source_target_pairs={{0,1},{1,0},{2,3},{3,2},{4,5},{5,4},{6,7},{7,6}} | collective-permute-start | bytes 30728 | tf_op jit(solution)/shard_map/ppermute | solution.py:877
  797.8 4.0 copy-start.4
  801.8 11.8 %copy-start.8 = (f32[1,1152]{1,0:T(1,128)S(1)}, f32[1,1152]{1,0:T(1,128)}, u32[]{:S(2)}) copy-start(f32[1,1152]{1,0:T(1,128)} %copy-done.7) | copy-start | bytes 13828
  801.8 11.9 %copy-start.16 = (bf16[512,1152]{1,0:T(8,128)(2,1)S(1)}, bf16[512,1152]{1,0:T(8,128)(2,1)}, u32[]{:S(2)}) copy-start(bf16[512,1152]{1,0:T(8,128)(2,1)} %copy-done.15) | copy-start | bytes 3538948
  813.6 14.1 %copy-start = (bf16[2048,2560]{1,0:T(8,128)(2,1)}, bf16[2048,2560]{1,0:T(8,128)(2,1)S(1)}, u32[]{:S(2)}) copy-start(bf16[2048,2560]{1,0:T(8,128)(2,1)S(1)} %d_soft.1.ds_ref.ds) | copy-start | bytes 31457284
  827.7 3.6 collective-permute-start.15
  829.0 5.3 collective-permute-start.23
  829.0 9.0 %collective-permute-start.24 = (bf16[512,2560]{1,0:T(8,128)(2,1)S(1)}, bf16[512,2560]{1,0:T(8,128)(2,1)}, u32[]{:S(2)}, u32[]{:S(2)}) collective-permute-start(bf16[512,2560]{1,0:T(8,128)(2,1)S(1)} %collective-permute-done.22.go_x), channel_id=1, source_target_pairs={{0,1},{1,0},{2,3},{3,2},{4,5},{5,4},{6,7},{7,6}} | collective-permute-start | bytes 7864328 | tf_op jit(solution)/shard_map/ppermute | solution.py:877
  829.6 12.2 %collective-permute-start.18 = (bf16[1280,1024]{1,0:T(8,128)(2,1)}, bf16[1280,1024]{1,0:T(8,128)(2,1)}, u32[]{:S(2)}, u32[]{:S(2)}) collective-permute-start(bf16[1280,1024]{1,0:T(8,128)(2,1)} %get-tuple-element.126), channel_id=1, source_target_pairs={{0,1},{1,0},{2,3},{3,2},{4,5},{5,4},{6,7},{7,6}} | collective-permute-start | bytes 7864328 | tf_op jit(solution)/shard_map/ppermute | solution.py:877
  831.3 14.3 %collective-permute-start.19 = (bf16[1280,1024]{1,0:T(8,128)(2,1)}, bf16[1280,1024]{1,0:T(8,128)(2,1)}, u32[]{:S(2)}, u32[]{:S(2)}) collective-permute-start(bf16[1280,1024]{1,0:T(8,128)(2,1)} %get-tuple-element.127), channel_id=1, source_target_pairs={{0,1},{1,0},{2,3},{3,2},{4,5},{5,4},{6,7},{7,6}} | collective-permute-start | bytes 7864328 | tf_op jit(solution)/shard_map/ppermute | solution.py:877
  834.3 38.2 %collective-permute-start.16 = (f32[1,1152]{1,0:T(1,128)S(1)}, f32[1,1152]{1,0:T(1,128)S(1)}, u32[]{:S(2)}, u32[]{:S(2)}) collective-permute-start(f32[1,1152]{1,0:T(1,128)S(1)} %add.94), channel_id=1, source_target_pairs={{0,1},{1,0},{2,3},{3,2},{4,5},{5,4},{6,7},{7,6}} | collective-permute-start | bytes 13832 | tf_op jit(solution)/shard_map/ppermute | solution.py:877
  845.5 2.3 copy-start.2
  (10 other events, 12.0 us)
